TPU v7x, 128 devices: a whole 4x4x4 slice. The times are simulated.
128 devices in a mesh: member: 16 (over x_lo, y, core), strip: 8 (over z, x_hi).
Axes of the slice: x: 4 (x_hi: 2, x_lo: 2; x = x_hi * 2 + x_lo), y: 4, z: 4, core: 2. Of those that a mesh axis runs over, the one named last changes fastest.
Arguments:
- sample_fields: float32 [64, 3, 128, 2048], P('member', None, 'strip'), may hold values from -0.8 to 0.8
- report_counts: int32 [8, 16], P('strip', 'member'), may hold values from 1 to 256, as said below
- report_cells: int32 [8, 16, 256], P('strip', 'member'), may hold values from 0 to 2047
- report_values: float32 [8, 16, 256], P('strip', 'member'), may hold values from -1.5 to 1.5
- report_errors: float32 [8, 16, 256], P('strip', 'member'), may hold values from 0.04 to 0.2
- local_radius: int32 [8, 16], P('strip', 'member'), may hold values from 1 to 3
Outputs:
- analysis: float32 [64, 3, 128, 2048], P('member', None, 'strip')
Inputs may be any that keep to these rules, and one draw needn't show every extreme that they name: `report_counts`: counts lie between 1 and 256; 256 is reached by some region in every draw; slots from the count on are not used.
All inputs are finite; a program needn't handle non-finite values.
Results may differ from a plain program's by a relative error of at most 0.0003.
Values sent between devices are 32-bit elements; how exact they have to be, the bound alone decides.
A program may use at most 64 MiB of HBM per device.

v0:
```python
import jax
import jax.numpy as jnp
from jax import lax
from jax.sharding import PartitionSpec as P

BAND_HEIGHT_CELLS = 16
PATCH_WIDTH_CELLS = 128
STEPS = 12
TURNS = 20


COURANT = 0.125
GRAVITY = 1.0
ROTATION = 0.05
HIGHEST_PRECISION = lax.Precision.HIGHEST


def with_halo(block, sides, width):
    for axis, dim in sides:
        count = lax.axis_size(axis)
        forward = [(i, i + 1) for i in range(count - 1)]
        forward.append((count - 1, 0))
        backward = [(target, source) for source, target in forward]
        low = lax.ppermute(
            lax.slice_in_dim(block, block.shape[dim] - width, None, axis=dim), axis, forward
        )
        high = lax.ppermute(lax.slice_in_dim(block, 0, width, axis=dim), axis, backward)
        block = jnp.concatenate([low, block, high], axis=dim)
    return block


def to_east(field):
    return field[..., 1:-1, 2:]


def to_west(field):
    return field[..., 1:-1, :-2]


def to_north(field):
    return field[..., 2:, 1:-1]


def to_south(field):
    return field[..., :-2, 1:-1]


def middle(field):
    return field[..., 1:-1, 1:-1]


def neighbour_mean(field):
    return 0.25 * (to_east(field) + to_west(field) + to_north(field) + to_south(field))


def advance_once(padded):
    height = padded[:, 0]
    flow_x = padded[:, 1]
    flow_y = padded[:, 2]
    column_depth = 1.0 + height
    flux_x = column_depth * flow_x
    flux_y = column_depth * flow_y
    centre_x = middle(flow_x)
    centre_y = middle(flow_y)
    new_height = neighbour_mean(height) - COURANT * (
        to_east(flux_x) - to_west(flux_x) + to_north(flux_y) - to_south(flux_y)
    )
    new_flow_x = (
        neighbour_mean(flow_x)
        - COURANT
        * (
            centre_x * (to_east(flow_x) - to_west(flow_x))
            + centre_y * (to_north(flow_x) - to_south(flow_x))
            + GRAVITY * (to_east(height) - to_west(height))
        )
        + ROTATION * centre_y
    )
    new_flow_y = (
        neighbour_mean(flow_y)
        - COURANT
        * (
            centre_x * (to_east(flow_y) - to_west(flow_y))
            + centre_y * (to_north(flow_y) - to_south(flow_y))
            + GRAVITY * (to_north(height) - to_south(height))
        )
        - ROTATION * centre_x
    )
    return jnp.stack([new_height, new_flow_x, new_flow_y], axis=1)


def observe(region, locations, values, errors, live_count):
    observed = jnp.take(region, locations, axis=1)
    observed_mean = jnp.mean(observed, axis=0)
    spread = observed - observed_mean[None, :]
    innovation = values - observed_mean
    slot_ids = jnp.arange(locations.shape[0])
    precision = jnp.where(slot_ids < live_count, 1.0 / errors, 0.0 * errors)
    row_pos = ((locations // PATCH_WIDTH_CELLS).astype(jnp.float32) + 0.5) / BAND_HEIGHT_CELLS - 0.5
    col_pos = ((locations % PATCH_WIDTH_CELLS).astype(jnp.float32) + 0.5) / PATCH_WIDTH_CELLS - 0.5
    return jnp.concatenate(
        [spread, innovation[None], precision[None], row_pos[None], col_pos[None]], axis=0
    )


def analyse(region, neighbours, radius_blocks):
    sample_collection = region.shape[0]
    offsets = jnp.arange(3).astype(region.dtype) - 1.0
    anomalies = neighbours[:, :, :sample_collection, :]
    innovation = neighbours[:, :, sample_collection, :].reshape(-1)
    precision = neighbours[:, :, sample_collection + 1, :]
    row_pos = neighbours[:, :, sample_collection + 2, :] + offsets[:, None, None]
    col_pos = neighbours[:, :, sample_collection + 3, :] + offsets[None, :, None]
    radius_float = radius_blocks.astype(region.dtype)
    tapering = jnp.exp(
        -0.5 * (row_pos * row_pos + col_pos * col_pos) / (radius_float * radius_float)
    )
    weights = (tapering * precision).reshape(-1)
    spread = jnp.transpose(anomalies, (2, 0, 1, 3)).reshape(sample_collection, -1)
    weighted = spread * weights[None, :]
    ensemble_scale = sample_collection - 1.0
    identity = jnp.eye(sample_collection, dtype=region.dtype)
    gram_matrix = jnp.dot(weighted, spread.T, precision=HIGHEST_PRECISION)
    normal = identity + gram_matrix / ensemble_scale
    pull_vector = jnp.dot(weighted, innovation, precision=HIGHEST_PRECISION)
    frob_norm = jnp.sqrt(jnp.sum(normal * normal))
    iterate = normal / frob_norm
    inverse_root = identity
    for newton_turn in range(TURNS):
        factor = 1.5 * identity - 0.5 * jnp.dot(inverse_root, iterate, precision=HIGHEST_PRECISION)
        iterate = jnp.dot(iterate, factor, precision=HIGHEST_PRECISION)
        inverse_root = jnp.dot(factor, inverse_root, precision=HIGHEST_PRECISION)
    root_inverse = inverse_root / jnp.sqrt(frob_norm)
    full_inverse = jnp.dot(inverse_root, inverse_root, precision=HIGHEST_PRECISION) / frob_norm
    mean_weights = jnp.dot(full_inverse, pull_vector, precision=HIGHEST_PRECISION) / ensemble_scale
    transform = root_inverse + mean_weights[:, None]
    centre = jnp.mean(region, axis=0)
    deviations = region - centre[None, :]
    return centre[None, :] + jnp.dot(transform.T, deviations, precision=HIGHEST_PRECISION)


def strip_block(current_state, halo_depth):
    padded = with_halo(current_state, (("strip", 2),), halo_depth)
    padded = jnp.concatenate([padded[..., -halo_depth:], padded, padded[..., :halo_depth]], axis=3)
    for repeat in range(halo_depth):
        padded = advance_once(padded)
    return padded


def on_device(
    sample_fields, report_counts, report_cells, report_values, report_errors, local_radius
):
    own_members, fields, row_count, grid_cols = sample_fields.shape
    blocks = lax.axis_size("member")
    region_cols = grid_cols // blocks
    sample_collection = own_members * blocks
    halo_depth = 3
    rounds = STEPS // halo_depth

    def strip_round(counter, carried):
        return strip_block(carried, halo_depth)

    current_state = lax.fori_loop(0, rounds, strip_round, sample_fields)
    by_block = current_state.reshape(own_members, fields, row_count, blocks, region_cols)
    current_state = lax.all_to_all(by_block, "member", split_axis=3, concat_axis=0, tiled=True)
    region = current_state.reshape(sample_collection, fields * row_count * region_cols)
    packed = observe(
        region, report_cells[0, 0], report_values[0, 0], report_errors[0, 0], report_counts[0, 0]
    )
    neighbours = with_halo(packed[None, None], (("member", 1), ("strip", 0)), 1)
    updated = analyse(region, neighbours, local_radius[0, 0])
    outgoing = updated.reshape(sample_collection, fields, row_count, 1, region_cols)
    returned = lax.all_to_all(outgoing, "member", split_axis=0, concat_axis=3, tiled=True)
    return returned.reshape(own_members, fields, row_count, grid_cols)


def solution(mesh):
    in_specs = (
        P("member", None, "strip", None),
        P("strip", "member"),
        P("strip", "member", None),
        P("strip", "member", None),
        P("strip", "member", None),
        P("strip", "member"),
    )
    out_specs = P("member", None, "strip", None)
    return jax.shard_map(
        on_device, mesh=mesh, in_specs=in_specs, out_specs=out_specs, check_vma=False
    )
```

profile of v0, /device:TPU:1, one launch (start us, length us, event | category | flops | bytes accessed | tf_op | source)
XLA Modules:
  0.0 248.0 jit_solution(4394028686227675844)
XLA Ops:
  1.5 145.5 %while.10 = (s32[]{:T(128)}, f32[4,3,16,2048]{3,2,0,1:T(8,128)S(1)}, s32[]{:T(128)}) while((s32[]{:T(128)}, f32[4,3,16,2048]{3,2,0,1:T(8,128)S(1)}, s32[]{:T(128)}) %tuple.56), condition=%wide.region_1.0_spmd, body=%wide.region_0.0_spmd.sunk | while | flops 20927520 | bytes 79989080 | solution.py:162
  1.7 7.1 %collective-permute-start = (f32[4,3,3,2048]{3,2,0,1:T(4,128)S(1)}, f32[4,3,3,2048]{3,2,0,1:T(4,128)S(1)}, u32[]{:S(2)}, u32[]{:S(2)}) collective-permute-start(f32[4,3,3,2048]{3,2,0,1:T(4,128)S(1)} %get-tuple-element.91), channel_id=1, source_target_pairs={{1,0},{2,1},{3,2},{4,3},{5,4},{6,5},{7,6},{0,7},{9,8},{10,9},{11,1... | collective-permute-start | bytes 884744 | tf_op jit(solution)/shard_map/while/body/eval_jaxpr/ppermute | solution.py:27
  8.8 7.8 %collective-permute-done = f32[4,3,3,2048]{3,2,0,1:T(4,128)S(1)} collective-permute-done((f32[4,3,3,2048]{3,2,0,1:T(4,128)S(1)}, f32[4,3,3,2048]{3,2,0,1:T(4,128)S(1)}, u32[]{:S(2)}, u32[]{:S(2)}) %collective-permute-start) | collective-permute-done | bytes 294944 | tf_op jit(solution)/shard_map/while/body/eval_jaxpr/ppermute | solution.py:27
  16.6 9.4 %collective-permute-done.1 = f32[4,3,3,2048]{3,2,0,1:T(4,128)S(1)} collective-permute-done((f32[4,3,3,2048]{3,2,0,1:T(4,128)S(1)}, f32[4,3,3,2048]{3,2,0,1:T(4,128)S(1)}, u32[]{:S(2)}, u32[]{:S(2)}) %collective-permute-start.1) | collective-permute-done | bytes 294944 | tf_op jit(solution)/shard_map/while/body/eval_jaxpr/ppermute | solution.py:24
  27.8 3.2 %concatenate.19 = f32[4,3,22,2054]{3,2,0,1:T(8,128)S(1)} concatenate(f32[4,3,22,3]{3,2,0,1:T(8,128)S(1)} %get-tuple-element.93, f32[4,3,22,2048]{3,2,0,1:T(8,128)} %copy-done, f32[4,3,22,3]{3,2,0,1:T(8,128)S(1)} %get-tuple-element.94), dimensions={3} | concatenate | bytes 4338048 | tf_op jit(solution)/shard_map/while/body/eval_jaxpr/concatenate | solution.py:143
  31.3 2.7 %add_multiply_fusion.12 = (f32[4,20,2052]{2,1,0:T(8,128)S(1)}, f32[4,20,2052]{2,1,0:T(8,128)S(1)}, f32[4,20,2052]{2,1,0:T(8,128)S(1)}) fusion(f32[4,22,2054]{2,1,0:T(8,128)S(1)} %get-tuple-element.95, f32[4,22,2054]{2,1,0:T(8,128)S(1)} %get-tuple-element.96, f32[4,22,2054]{2,1,0:T(8,128)S(1)} %get-tuple-element.97, ...), kind=kLoop, calls=%fused_computation.23.clone.1 | loop fusion | flops 4268160 | bytes 11162880 | tf_op jit(solution)/shard_map/while/body/eval_jaxpr/mul | solution.py:61
  34.0 1.6 add_multiply_fusion.13
  35.6 2.7 %add_multiply_fusion.14 = (f32[4,18,2050]{2,1,0:T(8,128)S(1)}, f32[4,18,2050]{2,1,0:T(8,128)S(1)}, f32[4,18,2050]{2,1,0:T(8,128)S(1)}) fusion(f32[4,20,2052]{2,1,0:T(8,128)S(1)} %get-tuple-element.101, f32[4,20,2052]{2,1,0:T(8,128)S(1)} %get-tuple-element.102, f32[4,20,2052]{2,1,0:T(8,128)S(1)} %get-tuple-element.100, ...), kind=kLoop, calls=%fused_computation.21.clone.1 | loop fusion | flops 3837600 | bytes 10036800 | tf_op jit(solution)/shard_map/while/body/eval_jaxpr/mul | solution.py:61
  38.3 1.6 add_multiply_fusion.15
  40.8 1.6 add_bitcast_fusion.2
  42.8 2.7 %collective-permute-start = (f32[4,3,3,2048]{3,2,0,1:T(4,128)S(1)}, f32[4,3,3,2048]{3,2,0,1:T(4,128)S(1)}, u32[]{:S(2)}, u32[]{:S(2)}) collective-permute-start(f32[4,3,3,2048]{3,2,0,1:T(4,128)S(1)} %get-tuple-element.91), channel_id=1, source_target_pairs={{1,0},{2,1},{3,2},{4,3},{5,4},{6,5},{7,6},{0,7},{9,8},{10,9},{11,1... | collective-permute-start | bytes 884744 | tf_op jit(solution)/shard_map/while/body/eval_jaxpr/ppermute | solution.py:27
  45.8 7.7 %collective-permute-done = f32[4,3,3,2048]{3,2,0,1:T(4,128)S(1)} collective-permute-done((f32[4,3,3,2048]{3,2,0,1:T(4,128)S(1)}, f32[4,3,3,2048]{3,2,0,1:T(4,128)S(1)}, u32[]{:S(2)}, u32[]{:S(2)}) %collective-permute-start) | collective-permute-done | bytes 294944 | tf_op jit(solution)/shard_map/while/body/eval_jaxpr/ppermute | solution.py:27
  53.5 8.3 %collective-permute-done.1 = f32[4,3,3,2048]{3,2,0,1:T(4,128)S(1)} collective-permute-done((f32[4,3,3,2048]{3,2,0,1:T(4,128)S(1)}, f32[4,3,3,2048]{3,2,0,1:T(4,128)S(1)}, u32[]{:S(2)}, u32[]{:S(2)}) %collective-permute-start.1) | collective-permute-done | bytes 294944 | tf_op jit(solution)/shard_map/while/body/eval_jaxpr/ppermute | solution.py:24
  63.6 3.2 %concatenate.19 = f32[4,3,22,2054]{3,2,0,1:T(8,128)S(1)} concatenate(f32[4,3,22,3]{3,2,0,1:T(8,128)S(1)} %get-tuple-element.93, f32[4,3,22,2048]{3,2,0,1:T(8,128)} %copy-done, f32[4,3,22,3]{3,2,0,1:T(8,128)S(1)} %get-tuple-element.94), dimensions={3} | concatenate | bytes 4338048 | tf_op jit(solution)/shard_map/while/body/eval_jaxpr/concatenate | solution.py:143
  67.1 2.7 %add_multiply_fusion.12 = (f32[4,20,2052]{2,1,0:T(8,128)S(1)}, f32[4,20,2052]{2,1,0:T(8,128)S(1)}, f32[4,20,2052]{2,1,0:T(8,128)S(1)}) fusion(f32[4,22,2054]{2,1,0:T(8,128)S(1)} %get-tuple-element.95, f32[4,22,2054]{2,1,0:T(8,128)S(1)} %get-tuple-element.96, f32[4,22,2054]{2,1,0:T(8,128)S(1)} %get-tuple-element.97, ...), kind=kLoop, calls=%fused_computation.23.clone.1 | loop fusion | flops 4268160 | bytes 11162880 | tf_op jit(solution)/shard_map/while/body/eval_jaxpr/mul | solution.py:61
  69.8 1.6 add_multiply_fusion.13
  71.4 2.7 %add_multiply_fusion.14 = (f32[4,18,2050]{2,1,0:T(8,128)S(1)}, f32[4,18,2050]{2,1,0:T(8,128)S(1)}, f32[4,18,2050]{2,1,0:T(8,128)S(1)}) fusion(f32[4,20,2052]{2,1,0:T(8,128)S(1)} %get-tuple-element.101, f32[4,20,2052]{2,1,0:T(8,128)S(1)} %get-tuple-element.102, f32[4,20,2052]{2,1,0:T(8,128)S(1)} %get-tuple-element.100, ...), kind=kLoop, calls=%fused_computation.21.clone.1 | loop fusion | flops 3837600 | bytes 10036800 | tf_op jit(solution)/shard_map/while/body/eval_jaxpr/mul | solution.py:61
  74.1 1.6 add_multiply_fusion.15
  76.6 1.6 add_bitcast_fusion.2
  78.5 2.4 collective-permute-start
  81.6 6.8 %collective-permute-done = f32[4,3,3,2048]{3,2,0,1:T(4,128)S(1)} collective-permute-done((f32[4,3,3,2048]{3,2,0,1:T(4,128)S(1)}, f32[4,3,3,2048]{3,2,0,1:T(4,128)S(1)}, u32[]{:S(2)}, u32[]{:S(2)}) %collective-permute-start) | collective-permute-done | bytes 294944 | tf_op jit(solution)/shard_map/while/body/eval_jaxpr/ppermute | solution.py:27
  88.4 8.0 %collective-permute-done.1 = f32[4,3,3,2048]{3,2,0,1:T(4,128)S(1)} collective-permute-done((f32[4,3,3,2048]{3,2,0,1:T(4,128)S(1)}, f32[4,3,3,2048]{3,2,0,1:T(4,128)S(1)}, u32[]{:S(2)}, u32[]{:S(2)}) %collective-permute-start.1) | collective-permute-done | bytes 294944 | tf_op jit(solution)/shard_map/while/body/eval_jaxpr/ppermute | solution.py:24
  98.2 3.2 %concatenate.19 = f32[4,3,22,2054]{3,2,0,1:T(8,128)S(1)} concatenate(f32[4,3,22,3]{3,2,0,1:T(8,128)S(1)} %get-tuple-element.93, f32[4,3,22,2048]{3,2,0,1:T(8,128)} %copy-done, f32[4,3,22,3]{3,2,0,1:T(8,128)S(1)} %get-tuple-element.94), dimensions={3} | concatenate | bytes 4338048 | tf_op jit(solution)/shard_map/while/body/eval_jaxpr/concatenate | solution.py:143
  101.7 2.7 %add_multiply_fusion.12 = (f32[4,20,2052]{2,1,0:T(8,128)S(1)}, f32[4,20,2052]{2,1,0:T(8,128)S(1)}, f32[4,20,2052]{2,1,0:T(8,128)S(1)}) fusion(f32[4,22,2054]{2,1,0:T(8,128)S(1)} %get-tuple-element.95, f32[4,22,2054]{2,1,0:T(8,128)S(1)} %get-tuple-element.96, f32[4,22,2054]{2,1,0:T(8,128)S(1)} %get-tuple-element.97, ...), kind=kLoop, calls=%fused_computation.23.clone.1 | loop fusion | flops 4268160 | bytes 11162880 | tf_op jit(solution)/shard_map/while/body/eval_jaxpr/mul | solution.py:61
  104.4 1.6 add_multiply_fusion.13
  106.0 2.7 %add_multiply_fusion.14 = (f32[4,18,2050]{2,1,0:T(8,128)S(1)}, f32[4,18,2050]{2,1,0:T(8,128)S(1)}, f32[4,18,2050]{2,1,0:T(8,128)S(1)}) fusion(f32[4,20,2052]{2,1,0:T(8,128)S(1)} %get-tuple-element.101, f32[4,20,2052]{2,1,0:T(8,128)S(1)} %get-tuple-element.102, f32[4,20,2052]{2,1,0:T(8,128)S(1)} %get-tuple-element.100, ...), kind=kLoop, calls=%fused_computation.21.clone.1 | loop fusion | flops 3837600 | bytes 10036800 | tf_op jit(solution)/shard_map/while/body/eval_jaxpr/mul | solution.py:61
  108.7 1.6 add_multiply_fusion.15
  111.2 1.6 add_bitcast_fusion.2
  113.2 2.4 collective-permute-start
  116.2 6.0 %collective-permute-done = f32[4,3,3,2048]{3,2,0,1:T(4,128)S(1)} collective-permute-done((f32[4,3,3,2048]{3,2,0,1:T(4,128)S(1)}, f32[4,3,3,2048]{3,2,0,1:T(4,128)S(1)}, u32[]{:S(2)}, u32[]{:S(2)}) %collective-permute-start) | collective-permute-done | bytes 294944 | tf_op jit(solution)/shard_map/while/body/eval_jaxpr/ppermute | solution.py:27
  122.2 8.1 %collective-permute-done.1 = f32[4,3,3,2048]{3,2,0,1:T(4,128)S(1)} collective-permute-done((f32[4,3,3,2048]{3,2,0,1:T(4,128)S(1)}, f32[4,3,3,2048]{3,2,0,1:T(4,128)S(1)}, u32[]{:S(2)}, u32[]{:S(2)}) %collective-permute-start.1) | collective-permute-done | bytes 294944 | tf_op jit(solution)/shard_map/while/body/eval_jaxpr/ppermute | solution.py:24
  132.1 3.2 %concatenate.19 = f32[4,3,22,2054]{3,2,0,1:T(8,128)S(1)} concatenate(f32[4,3,22,3]{3,2,0,1:T(8,128)S(1)} %get-tuple-element.93, f32[4,3,22,2048]{3,2,0,1:T(8,128)} %copy-done, f32[4,3,22,3]{3,2,0,1:T(8,128)S(1)} %get-tuple-element.94), dimensions={3} | concatenate | bytes 4338048 | tf_op jit(solution)/shard_map/while/body/eval_jaxpr/concatenate | solution.py:143
  135.6 2.7 %add_multiply_fusion.12 = (f32[4,20,2052]{2,1,0:T(8,128)S(1)}, f32[4,20,2052]{2,1,0:T(8,128)S(1)}, f32[4,20,2052]{2,1,0:T(8,128)S(1)}) fusion(f32[4,22,2054]{2,1,0:T(8,128)S(1)} %get-tuple-element.95, f32[4,22,2054]{2,1,0:T(8,128)S(1)} %get-tuple-element.96, f32[4,22,2054]{2,1,0:T(8,128)S(1)} %get-tuple-element.97, ...), kind=kLoop, calls=%fused_computation.23.clone.1 | loop fusion | flops 4268160 | bytes 11162880 | tf_op jit(solution)/shard_map/while/body/eval_jaxpr/mul | solution.py:61
  138.3 1.6 add_multiply_fusion.13
  139.9 2.7 %add_multiply_fusion.14 = (f32[4,18,2050]{2,1,0:T(8,128)S(1)}, f32[4,18,2050]{2,1,0:T(8,128)S(1)}, f32[4,18,2050]{2,1,0:T(8,128)S(1)}) fusion(f32[4,20,2052]{2,1,0:T(8,128)S(1)} %get-tuple-element.101, f32[4,20,2052]{2,1,0:T(8,128)S(1)} %get-tuple-element.102, f32[4,20,2052]{2,1,0:T(8,128)S(1)} %get-tuple-element.100, ...), kind=kLoop, calls=%fused_computation.21.clone.1 | loop fusion | flops 3837600 | bytes 10036800 | tf_op jit(solution)/shard_map/while/body/eval_jaxpr/mul | solution.py:61
  142.6 1.6 add_multiply_fusion.15
  145.1 1.6 add_bitcast_fusion.2
  147.4 1.6 copy.23
  149.0 9.5 %all-to-all-start = ((f32[4,3,16,16,128]{4,2,1,0,3:T(8,128)}), f32[4,3,16,16,128]{4,2,1,0,3:T(8,128)S(1)}, u32[]{:S(2)}, u32[]{:S(2)}) async-start(f32[4,3,16,16,128]{4,2,1,0,3:T(8,128)} %copy.23), calls=%async_computation | async-start | bytes 3145728 | tf_op jit(solution)/shard_map/all_to_all | solution.py:164
  159.9 19.9 %all-to-all-done = f32[4,3,16,16,128]{4,2,1,0,3:T(8,128)S(1)} async-done(((f32[4,3,16,16,128]{4,2,1,0,3:T(8,128)}), f32[4,3,16,16,128]{4,2,1,0,3:T(8,128)S(1)}, u32[]{:S(2)}, u32[]{:S(2)}) %all-to-all-start) | async-done | bytes 1572896 | tf_op jit(solution)/shard_map/all_to_all | solution.py:164
  180.1 2.3 copy.24
  182.4 2.6 %gather_fusion = f32[256,64]{1,0:T(8,128)S(1)} fusion(f32[64,6144]{0,1:T(8,128)} %copy.24, s32[1024]{0:T(1024)S(1)} %pad_clamp_fusion), kind=kCustom, calls=%fused_computation | custom fusion | bytes 132096 | tf_op jit(solution)/shard_map/jit(_take)/gather | solution.py:92
  187.0 2.1 collective-permute-done.3
  189.1 2.5 %collective-permute-start.4 = (f32[1,3,68,256]{3,2,1,0:T(8,128)S(1)}, f32[1,3,68,256]{3,2,1,0:T(8,128)S(1)}, u32[]{:S(2)}, u32[]{:S(2)}) collective-permute-start(f32[1,3,68,256]{3,2,1,0:T(8,128)S(1)} %pad_maximum_fusion.3), channel_id=1, source_target_pairs={{0,1},{1,2},{2,3},{3,4},{4,5},{5,6},{6,7},{7,0},{8,9},{9,10},{10,1... | collective-permute-start | bytes 626696 | tf_op jit(solution)/shard_map/ppermute | solution.py:24
  191.6 3.6 %collective-permute-start.5 = (f32[1,3,68,256]{3,2,1,0:T(8,128)S(1)}, f32[1,3,68,256]{3,2,1,0:T(8,128)S(1)}, u32[]{:S(2)}, u32[]{:S(2)}) collective-permute-start(f32[1,3,68,256]{3,2,1,0:T(8,128)S(1)} %pad_maximum_fusion.3), channel_id=1, source_target_pairs={{1,0},{2,1},{3,2},{4,3},{5,4},{6,5},{7,6},{0,7},{9,8},{10,9},{11,1... | collective-permute-start | bytes 626696 | tf_op jit(solution)/shard_map/ppermute | solution.py:27
  195.2 4.0 %collective-permute-done.4 = f32[1,3,68,256]{3,2,1,0:T(8,128)S(1)} collective-permute-done((f32[1,3,68,256]{3,2,1,0:T(8,128)S(1)}, f32[1,3,68,256]{3,2,1,0:T(8,128)S(1)}, u32[]{:S(2)}, u32[]{:S(2)}) %collective-permute-start.4) | collective-permute-done | bytes 208928 | tf_op jit(solution)/shard_map/ppermute | solution.py:24
  214.7 1.6 fusion.8
  216.6 29.0 %all_to_all.30 = f32[64,3,16,1,128]{4,2,1,3,0:T(8,128)S(1)} all-to-all(f32[64,3,16,1,128]{4,2,1,3,0:T(8,128)S(1)} %bitcast.264), channel_id=1, replica_groups=mesh['member'=16,'strip'=8] {'member'}, dimensions={0} | all-to-all | bytes 3145728 | tf_op jit(solution)/shard_map/all_to_all | solution.py:172
  (141 shorter events, 35.8 us)
Async XLA Ops:
  1.7 14.9 %collective-permute-start = (f32[4,3,3,2048]{3,2,0,1:T(4,128)S(1)}, f32[4,3,3,2048]{3,2,0,1:T(4,128)S(1)}, u32[]{:S(2)}, u32[]{:S(2)}) collective-permute-start(f32[4,3,3,2048]{3,2,0,1:T(4,128)S(1)} %get-tuple-element.91), channel_id=1, source_target_pairs={{1,0},{2,1},{3,2},{4,3},{5,4},{6,5},{7,6},{0,7},{9,8},{10,9},{11,1... | collective-permute-start | bytes 884744 | tf_op jit(solution)/shard_map/while/body/eval_jaxpr/ppermute | solution.py:27
  8.8 17.2 %collective-permute-start.1 = (f32[4,3,3,2048]{3,2,0,1:T(4,128)S(1)}, f32[4,3,3,2048]{3,2,0,1:T(4,128)S(1)}, u32[]{:S(2)}, u32[]{:S(2)}) collective-permute-start(f32[4,3,3,2048]{3,2,0,1:T(4,128)S(1)} %get-tuple-element.92), channel_id=1, source_target_pairs={{0,1},{1,2},{2,3},{3,4},{4,5},{5,6},{6,7},{7,0},{8,9},{9,10},{10,1... | collective-permute-start | bytes 884744 | tf_op jit(solution)/shard_map/while/body/eval_jaxpr/ppermute | solution.py:24
  26.3 1.4 copy-start
  42.8 10.7 %collective-permute-start = (f32[4,3,3,2048]{3,2,0,1:T(4,128)S(1)}, f32[4,3,3,2048]{3,2,0,1:T(4,128)S(1)}, u32[]{:S(2)}, u32[]{:S(2)}) collective-permute-start(f32[4,3,3,2048]{3,2,0,1:T(4,128)S(1)} %get-tuple-element.91), channel_id=1, source_target_pairs={{1,0},{2,1},{3,2},{4,3},{5,4},{6,5},{7,6},{0,7},{9,8},{10,9},{11,1... | collective-permute-start | bytes 884744 | tf_op jit(solution)/shard_map/while/body/eval_jaxpr/ppermute | solution.py:27
  45.4 16.3 %collective-permute-start.1 = (f32[4,3,3,2048]{3,2,0,1:T(4,128)S(1)}, f32[4,3,3,2048]{3,2,0,1:T(4,128)S(1)}, u32[]{:S(2)}, u32[]{:S(2)}) collective-permute-start(f32[4,3,3,2048]{3,2,0,1:T(4,128)S(1)} %get-tuple-element.92), channel_id=1, source_target_pairs={{0,1},{1,2},{2,3},{3,4},{4,5},{5,6},{6,7},{7,0},{8,9},{9,10},{10,1... | collective-permute-start | bytes 884744 | tf_op jit(solution)/shard_map/while/body/eval_jaxpr/ppermute | solution.py:24
  62.1 1.4 copy-start
  78.5 9.9 %collective-permute-start = (f32[4,3,3,2048]{3,2,0,1:T(4,128)S(1)}, f32[4,3,3,2048]{3,2,0,1:T(4,128)S(1)}, u32[]{:S(2)}, u32[]{:S(2)}) collective-permute-start(f32[4,3,3,2048]{3,2,0,1:T(4,128)S(1)} %get-tuple-element.91), channel_id=1, source_target_pairs={{1,0},{2,1},{3,2},{4,3},{5,4},{6,5},{7,6},{0,7},{9,8},{10,9},{11,1... | collective-permute-start | bytes 884744 | tf_op jit(solution)/shard_map/while/body/eval_jaxpr/ppermute | solution.py:27
  80.9 15.5 %collective-permute-start.1 = (f32[4,3,3,2048]{3,2,0,1:T(4,128)S(1)}, f32[4,3,3,2048]{3,2,0,1:T(4,128)S(1)}, u32[]{:S(2)}, u32[]{:S(2)}) collective-permute-start(f32[4,3,3,2048]{3,2,0,1:T(4,128)S(1)} %get-tuple-element.92), channel_id=1, source_target_pairs={{0,1},{1,2},{2,3},{3,4},{4,5},{5,6},{6,7},{7,0},{8,9},{9,10},{10,1... | collective-permute-start | bytes 884744 | tf_op jit(solution)/shard_map/while/body/eval_jaxpr/ppermute | solution.py:24
  96.7 1.4 copy-start
  113.2 9.0 %collective-permute-start = (f32[4,3,3,2048]{3,2,0,1:T(4,128)S(1)}, f32[4,3,3,2048]{3,2,0,1:T(4,128)S(1)}, u32[]{:S(2)}, u32[]{:S(2)}) collective-permute-start(f32[4,3,3,2048]{3,2,0,1:T(4,128)S(1)} %get-tuple-element.91), channel_id=1, source_target_pairs={{1,0},{2,1},{3,2},{4,3},{5,4},{6,5},{7,6},{0,7},{9,8},{10,9},{11,1... | collective-permute-start | bytes 884744 | tf_op jit(solution)/shard_map/while/body/eval_jaxpr/ppermute | solution.py:27
  115.5 14.7 %collective-permute-start.1 = (f32[4,3,3,2048]{3,2,0,1:T(4,128)S(1)}, f32[4,3,3,2048]{3,2,0,1:T(4,128)S(1)}, u32[]{:S(2)}, u32[]{:S(2)}) collective-permute-start(f32[4,3,3,2048]{3,2,0,1:T(4,128)S(1)} %get-tuple-element.92), channel_id=1, source_target_pairs={{0,1},{1,2},{2,3},{3,4},{4,5},{5,6},{6,7},{7,0},{8,9},{9,10},{10,1... | collective-permute-start | bytes 884744 | tf_op jit(solution)/shard_map/while/body/eval_jaxpr/ppermute | solution.py:24
  130.6 1.4 copy-start
  149.0 10.8 %copy-start.1 = (s32[1,1,256]{2,1,0:T(1,128)S(1)}, s32[1,1,256]{2,1,0:T(1,128)}, u32[]{:S(2)}) copy-start(s32[1,1,256]{2,1,0:T(1,128)} %param.10) | copy-start | bytes 3076
  149.0 10.9 %copy-start.3 = (f32[1,1,256]{2,1,0:T(1,128)S(1)}, f32[1,1,256]{2,1,0:T(1,128)}, u32[]{:S(2)}) copy-start(f32[1,1,256]{2,1,0:T(1,128)} %param.12) | copy-start | bytes 3076
  149.0 30.9 %all-to-all-start = ((f32[4,3,16,16,128]{4,2,1,0,3:T(8,128)}), f32[4,3,16,16,128]{4,2,1,0,3:T(8,128)S(1)}, u32[]{:S(2)}, u32[]{:S(2)}) async-start(f32[4,3,16,16,128]{4,2,1,0,3:T(8,128)} %copy.23), calls=%async_computation | async-start | bytes 3145728 | tf_op jit(solution)/shard_map/all_to_all | solution.py:164
  180.1 5.0 %copy-start.2 = (f32[1,1,256]{2,1,0:T(1,128)S(1)}, f32[1,1,256]{2,1,0:T(1,128)}, u32[]{:S(2)}) copy-start(f32[1,1,256]{2,1,0:T(1,128)} %param.11) | copy-start | bytes 3076
  185.2 1.8 collective-permute-start.2
  185.3 3.8 %collective-permute-start.3 = (f32[1,1,68,256]{3,2,1,0:T(8,128)S(1)}, f32[1,1,68,256]{3,2,1,0:T(8,128)S(1)}, u32[]{:S(2)}, u32[]{:S(2)}) collective-permute-start(f32[1,1,68,256]{3,2,1,0:T(8,128)S(1)} %bitcast.267), channel_id=1, source_target_pairs={{8,0},{16,8},{24,16},{32,24},{40,32},{48,40},{56,48},{64,56},{72,6... | collective-permute-start | bytes 208904 | tf_op jit(solution)/shard_map/ppermute | solution.py:27
  189.1 10.1 %collective-permute-start.4 = (f32[1,3,68,256]{3,2,1,0:T(8,128)S(1)}, f32[1,3,68,256]{3,2,1,0:T(8,128)S(1)}, u32[]{:S(2)}, u32[]{:S(2)}) collective-permute-start(f32[1,3,68,256]{3,2,1,0:T(8,128)S(1)} %pad_maximum_fusion.3), channel_id=1, source_target_pairs={{0,1},{1,2},{2,3},{3,4},{4,5},{5,6},{6,7},{7,0},{8,9},{9,10},{10,1... | collective-permute-start | bytes 626696 | tf_op jit(solution)/shard_map/ppermute | solution.py:24
  191.6 9.1 %collective-permute-start.5 = (f32[1,3,68,256]{3,2,1,0:T(8,128)S(1)}, f32[1,3,68,256]{3,2,1,0:T(8,128)S(1)}, u32[]{:S(2)}, u32[]{:S(2)}) collective-permute-start(f32[1,3,68,256]{3,2,1,0:T(8,128)S(1)} %pad_maximum_fusion.3), channel_id=1, source_target_pairs={{1,0},{2,1},{3,2},{4,3},{5,4},{6,5},{7,6},{0,7},{9,8},{10,9},{11,1... | collective-permute-start | bytes 626696 | tf_op jit(solution)/shard_map/ppermute | solution.py:27
where the time goes:
time: 249 us; the launch traced here: 248 us
  waiting for transfers between devices  90.2 us (36%)
  other arithmetic  47.4 us (19%)
  starting transfers between devices  32.9 us (13%)
  local copies, waits for them, and re-layouts  31.8 us (13%)
  blocking collectives  29 us (12%)
  matrix products  13.3 us (5%)
  between operations  2.71 us (1%)
    ppermute x6, waiting for transfers between devices, with_halo(): lax.ppermute(lax.slice_in_dim(block, block.shape[dim] - width, None, axis...  38.3 us
    ppermute x6, waiting for transfers between devices, with_halo(): lax.ppermute(lax.slice_in_dim(block, 0, width, axis=dim), axis, backward)  31.9 us
    all_to_all x1, blocking collectives, on_device(): lax.all_to_all(outgoing, 'member', split_axis=0, concat_axis=3, tiled=True)  29 us
    mul x12, other arithmetic, advance_once(): flux_x = column_depth * flow_x  21.9 us
    all_to_all x1, waiting for transfers between devices, on_device(): lax.all_to_all(by_block, 'member', split_axis=3, concat_axis=0, tiled=True)  19.9 us
    ppermute x6, starting transfers between devices, with_halo(): lax.ppermute(lax.slice_in_dim(block, 0, width, axis=dim), axis, backward)  19.1 us
    mul x8, other arithmetic, advance_once(): flux_y = column_depth * flow_y  12.9 us
    concatenate x4, local copies, waits for them, and re-layouts, strip_block(): jnp.concatenate([padded[..., -halo_depth:], padded, padded[..., :halo_dep...  12.9 us
  transfers between devices with their start and end apart: 13, of which 13 were waited for; matrix products, arithmetic and copies ran while one was open for 0% of the time, Pallas kernels for 0%

commit v1 on v0

v1 whole, which is shorter than its diff:
```python
import jax
import jax.numpy as jnp
from jax import lax
from jax.experimental import pallas as pl
from jax.experimental.pallas import tpu as pltpu
from jax.sharding import PartitionSpec as P

STEPS = 12
TURNS = 20
MEMBERS = 64
OWN = 4
STRIPS = 8
OWNERS = 16
ROWS = 16
COLS = 128
BLOCK = 256
OBS = 256
EDGE = 16
GUARD = 8
FIRST = GUARD + EDGE
SPAN = BLOCK + 2 * EDGE + 2 * GUARD
UNROLL = 6
MESH = pl.DeviceIdType.MESH
F32 = jnp.float32
BF16 = jnp.bfloat16


def block_of(strip):
    z, xh = strip // 2, strip % 2
    return z + xh * (7 - 2 * z)


def strip_of(block):
    return 2 * block + (block // 4) * (15 - 4 * block)


def region_of(i, strip):
    y, c, z = (i // 2) % 4, i % 2, strip // 2
    return 2 * ((y + z) % 4) + (c + y) % 2, i // 8


def owner_of(a, b):
    strip = strip_of(b // 2)
    y = (a // 2 + 4 - strip // 2) % 4
    return (b % 2) * 8 + y * 2 + (a + y) % 2, strip


def remote(src, dst, send, recv, where):
    return pltpu.make_async_remote_copy(
        src_ref=src, dst_ref=dst, send_sem=send, recv_sem=recv, device_id=where, device_id_type=MESH
    )


def halves(value):
    high = value.astype(BF16)
    return high, (value - high.astype(F32)).astype(BF16)


def thirds(value):
    high = value.astype(BF16)
    rest = value - high.astype(F32)
    mid = rest.astype(BF16)
    return high, mid, (rest - mid.astype(F32)).astype(BF16)


def dot(a, b):
    return jnp.dot(a, b, preferred_element_type=F32)


def matmul(a, b):
    ah, al = halves(a)
    bh, bl = halves(b)
    return dot(ah, bh) + (dot(ah, bl) + dot(al, bh))


def turn_north(value):
    return pltpu.roll(value, COLS - 1, 1)


def turn_south(value):
    return pltpu.roll(value, 1, 1)


def step_rows(src, dst, at):
    rows = pl.ds(at, 8)
    east, west = pl.ds(at + 1, 8), pl.ds(at - 1, 8)
    h, p, q = src[0, rows], src[1, rows], src[2, rows]
    he, pe, qe = src[0, east], src[1, east], src[2, east]
    hw, pw, qw = src[0, west], src[1, west], src[2, west]
    a, a2, b, b2 = 0.25 - p, 0.25 + p, 0.25 - q, 0.25 + q
    pn, ps = turn_north(p), turn_south(p)
    qn, qs = turn_north(q), turn_south(q)
    hn, hs = turn_north(h), turn_south(h)
    flow = (pe - pw) + (qn - qs)
    dst[0, rows] = (
        (he * (0.25 - pe) + hw * (0.25 + pw)) + (turn_north(h * b) + turn_south(h * b2))
    ) - (1.0 / 64.0) * flow
    dst[1, rows] = ((a * pe + a2 * pw) + (b * pn + b2 * ps)) + (0.05 * q - (he - hw))
    dst[2, rows] = ((a * qe + a2 * qw) + (b * qn + b2 * qs)) - (0.05 * p + (hn - hs))


def kernel(
    x, cells, values, errors, count, radius, out,
    landed, work, edge, halo, staged, region, mixed, packed, own, reach, near, onehot, tall_h, tall_l, roots, mix_h, mix_l, gram,
    grams,
    send1, recv1, send_edge, recv_edge, send2, recv2, send_obs, recv_obs, recv_reach,
    send_gram, recv_gram, send3, recv3,
):
    i = lax.axis_index("member")
    s = lax.axis_index("strip")
    t = block_of(s)
    a, b0 = region_of(i, s)
    b = 2 * t + b0

    for j in range(OWN):
        for d in range(1, STRIPS):
            to = lax.rem(s + d, STRIPS)
            remote(
                x.at[j, :, :, pl.ds(pl.multiple_of(block_of(to) * BLOCK, BLOCK), BLOCK)],
                landed.at[j, :, pl.ds(pl.multiple_of(s * ROWS, ROWS), ROWS)],
                send1.at[j], recv1.at[j], (i, to),
            ).start()
        pltpu.make_async_copy(
            x.at[j, :, :, pl.ds(pl.multiple_of(t * BLOCK, BLOCK), BLOCK)],
            landed.at[j, :, pl.ds(pl.multiple_of(s * ROWS, ROWS), ROWS)],
            recv1.at[j],
        ).start()

    slots = lax.broadcasted_iota(jnp.int32, (1, OBS), 1)
    packed[0:1] = cells[...].astype(F32)
    packed[1:2] = values[...]
    packed[2:3] = jnp.where(slots < count[0, 0], 1.0 / errors[...], 0.0)
    reach[...] = jnp.full((8, COLS), radius[0, 0], jnp.int32).astype(F32)
    to_i, to_s = owner_of(s, i)
    mine = (to_i == i) & (to_s == s)

    @pl.when(mine)
    def _():
        pltpu.make_async_copy(packed, own, recv_obs).start()

    @pl.when(jnp.logical_not(mine))
    def _():
        remote(packed, own, send_obs.at[9], recv_obs, (to_i, to_s)).start()

    def each_near(act_local, act_remote):
        for k in range(9):
            n_i, n_s = owner_of((s + k // 3 + 7) % 8, (i + k % 3 + 15) % 16)
            self = (n_i == i) & (n_s == s)
            if act_local is not None:
                pl.when(self)(lambda k=k: act_local(k))
            pl.when(jnp.logical_not(self))(lambda k=k, n_i=n_i, n_s=n_s: act_remote(k, n_i, n_s))

    each_near(
        lambda k: pltpu.make_async_copy(reach, near.at[k], recv_reach).start(),
        lambda k, n_i, n_s: remote(
            reach, near.at[k], send_obs.at[k], recv_reach, (n_i, n_s)
        ).start(),
    )

    left = (i, strip_of((t + 7) % 8))
    right = (i, strip_of((t + 1) % 8))
    for c in range(2):
        for g in range(2):
            for f in range(3):
                work[c, g, f, 0:GUARD] = jnp.zeros((GUARD, COLS), F32)
                work[c, g, f, SPAN - GUARD : SPAN] = jnp.zeros((GUARD, COLS), F32)

    def edge_copies(j):
        return (
            remote(
                edge.at[j, 0], halo.at[j, 1], send_edge.at[j, 0], recv_edge.at[j, 1], left
            ),
            remote(
                edge.at[j, 1], halo.at[j, 0], send_edge.at[j, 1], recv_edge.at[j, 0], right
            ),
        )

    def arrive(j):
        pltpu.make_async_copy(landed.at[j], landed.at[j], recv1.at[j]).wait()
        buf = work.at[j % 2, 0]
        for f in range(3):
            scale = 1.0 / 64.0 if f == 0 else 0.125
            for c in range(2):
                turned = landed[j, f, :, c * COLS : (c + 1) * COLS].T * scale
                buf[f, FIRST + c * COLS : FIRST + (c + 1) * COLS] = turned
                if c == 0:
                    edge[j, 0, f] = turned[:EDGE]
                else:
                    edge[j, 1, f] = turned[COLS - EDGE :]
        for copy in edge_copies(j):
            copy.start()

    def forecast(j):
        for copy in edge_copies(j):
            copy.wait_recv()
        ping, pong = work.at[j % 2, 0], work.at[j % 2, 1]
        for f in range(3):
            ping[f, GUARD:FIRST] = halo[j, 0, f]
            ping[f, FIRST + BLOCK : FIRST + BLOCK + EDGE] = halo[j, 1, f]

        def sweep(src, dst):
            def chunk(n, _):
                at = pl.multiple_of(n * (8 * UNROLL), 8) + GUARD
                for u in range(UNROLL):
                    step_rows(src, dst, at + 8 * u)
                return 0

            lax.fori_loop(0, (SPAN - 2 * GUARD) // (8 * UNROLL), chunk, 0)

        def two_steps(n, _):
            sweep(ping, pong)
            sweep(pong, ping)
            return 0

        lax.fori_loop(0, STEPS // 2, two_steps, 0)
        for f in range(3):
            scale = 64.0 if f == 0 else 8.0
            for c in range(2):
                block = ping[f, FIRST + c * COLS : FIRST + (c + 1) * COLS]
                staged[j, f, :, c * COLS : (c + 1) * COLS] = block.T * scale
        for d in range(OWNERS):
            to = lax.rem(i + d, OWNERS)
            to_a, to_b0 = region_of(to, s)
            src = staged.at[
                j, :, pl.ds(pl.multiple_of(to_a * ROWS, ROWS), ROWS),
                pl.ds(pl.multiple_of(to_b0 * COLS, COLS), COLS),
            ]
            dst = region.at[:, :, OWN * i + j]
            if d == 0:
                pltpu.make_async_copy(src, dst, recv2).start()
            else:
                remote(src, dst, send2, recv2, (to, s)).start()

    arrive(0)
    arrive(1)
    pltpu.make_async_copy(own, own, recv_obs).wait()
    place = own[0:1]

    def mark(n, _):
        at = pl.multiple_of(n * COLS, COLS)
        cell = lax.broadcasted_iota(jnp.int32, (COLS, OBS), 0) + at
        onehot[pl.ds(at, COLS)] = jnp.where(cell.astype(F32) == place, 1.0, 0.0).astype(BF16)
        return 0

    lax.fori_loop(0, ROWS, mark, 0)
    forecast(0)
    arrive(2)
    forecast(1)
    arrive(3)
    forecast(2)
    forecast(3)

    pltpu.make_async_copy(region, region, recv2).wait()

    def look(n, height):
        pair = jnp.concatenate([region[0, 2 * n], region[0, 2 * n + 1]], axis=1)
        marks = onehot[pl.ds(pl.multiple_of(n * OBS, OBS), OBS)]
        high, mid, low = thirds(pair)
        return height + (dot(high, marks) + (dot(mid, marks) + dot(low, marks)))

    height = lax.fori_loop(0, ROWS // 2, look, jnp.zeros((MEMBERS, OBS), F32))
    mean = jnp.mean(height, axis=0, keepdims=True)
    spread = height - mean
    innovation = own[1:2] - mean
    precision = own[2:3]
    line = jnp.floor(place * (1.0 / COLS))
    row_pos = (line + 0.5) * (1.0 / ROWS) - 0.5
    col_pos = (place - line * COLS + 0.5) * (1.0 / COLS) - 0.5
    wide = jnp.concatenate(
        [spread, innovation, jnp.zeros((COLS - MEMBERS - 1, OBS), F32)], axis=0
    )
    tall = jnp.concatenate([wide[:, :COLS].T, wide[:, COLS:].T], axis=0)
    columns_h, columns_l = halves(tall)
    tall_h[...], tall_l[...] = columns_h, columns_l
    pltpu.make_async_copy(near, near, recv_reach).wait()

    def product(k, _):
        r = row_pos + (k // 3 - 1).astype(F32)
        c = col_pos + (k % 3 - 1).astype(F32)
        radius_k = near[k, 0:1, 0:1]
        taper = jnp.exp(-0.5 * (r * r + c * c) / (radius_k * radius_k))
        wh, wl = halves(spread * (taper * precision))
        gram[k] = dot(wh, tall_h[...]) + (dot(wh, tall_l[...]) + dot(wl, tall_h[...]))
        return 0

    lax.fori_loop(0, 9, product, 0)

    def gram_copy(k):
        to = owner_of((a + 9 - k // 3) % 8, (b + 17 - k % 3) % 16)
        return remote(gram.at[k], grams.at[k], send_gram.at[k], recv_gram.at[k], to)

    for k in range(9):
        if k != 4:
            gram_copy(k).start()
    total = gram[4]
    for k in range(9):
        if k != 4:
            gram_copy(k).wait_recv()
            total = total + grams[k]

    scale = 1.0 / (MEMBERS - 1.0)
    eye = (
        lax.broadcasted_iota(jnp.int32, (MEMBERS, MEMBERS), 0)
        == lax.broadcasted_iota(jnp.int32, (MEMBERS, MEMBERS), 1)
    ).astype(F32)
    normal = eye + total[:, :MEMBERS] * scale
    frob2 = jnp.sum(jnp.sum(normal * normal, axis=1, keepdims=True), axis=0, keepdims=True)
    frob = jnp.sqrt(frob2)

    roots[0], roots[1] = normal / frob, eye

    def turn(_, carry):
        u, z = roots[0], roots[1]
        factor = 1.5 * eye - 0.5 * matmul(z, u)
        roots[0], roots[1] = matmul(u, factor), matmul(factor, z)
        return carry

    lax.fori_loop(0, TURNS, turn, 0)
    inverse = roots[1]
    pull = matmul(inverse, matmul(inverse, total)) / frob
    lane = lax.broadcasted_iota(jnp.int32, (MEMBERS, COLS), 1)
    mean_weights = jnp.sum(jnp.where(lane == MEMBERS, pull, 0.0), axis=1, keepdims=True) * scale
    transform = inverse / jnp.sqrt(frob) + mean_weights
    padded = jnp.concatenate(
        [
            jnp.concatenate([transform, jnp.zeros((MEMBERS, MEMBERS), F32)], axis=1),
            jnp.zeros((MEMBERS, COLS), F32),
        ],
        axis=0,
    )
    weights_h, weights_l = halves(padded.T[:MEMBERS])
    mix_h[...], mix_l[...] = weights_h, weights_l

    here = a == s
    columns = pl.ds(pl.multiple_of(b * COLS, COLS), COLS)
    for f in range(3):

        def rows_of(n, _):
            pair = jnp.concatenate([region[f, 2 * n], region[f, 2 * n + 1]], axis=1)
            centre = jnp.mean(pair, axis=0, keepdims=True)
            dev_h, dev_l = halves(pair - centre)
            result = centre + (
                dot(mix_h[:, :MEMBERS], dev_h)
                + (dot(mix_h[:, :MEMBERS], dev_l) + dot(mix_l[:, :MEMBERS], dev_h))
            )
            mixed[f, 2 * n] = result[:, :COLS]
            mixed[f, 2 * n + 1] = result[:, COLS:]
            return 0

        lax.fori_loop(0, ROWS // 2, rows_of, 0)
        for d in range(OWNERS):
            to = lax.rem(i + d, OWNERS)
            for j in range(OWN):
                src = mixed.at[f, :, OWN * to + j]
                dst = out.at[j, f, :, columns]
                if d == 0:
                    pl.when(here)(
                        lambda src=src, dst=dst: pltpu.make_async_copy(
                            src, dst, recv3
                        ).start()
                    )
                    pl.when(jnp.logical_not(here))(
                        lambda src=src, dst=dst: remote(
                            src, dst, send3.at[1], recv3, (i, a)
                        ).start()
                    )
                else:
                    remote(src, dst, send3.at[0], recv3, (to, a)).start()

    for j in range(OWN):
        rest = landed.at[j, :, pl.ds(0, ROWS * (STRIPS - 1))]
        remote(rest, rest, send1.at[j], recv1.at[j], (i, s)).wait_send()
        for copy in edge_copies(j):
            copy.wait_send()
    pl.when(jnp.logical_not(mine))(
        lambda: remote(packed, own, send_obs.at[9], recv_obs, (i, s)).wait_send()
    )
    each_near(
        None,
        lambda k, n_i, n_s: remote(
            reach, near.at[k], send_obs.at[k], recv_reach, (n_i, n_s)
        ).wait_send(),
    )
    rest = region.at[:, :, pl.ds(0, OWN * (OWNERS - 1))]
    remote(rest, rest, send2, recv2, (i, s)).wait_send()
    for k in range(9):
        if k != 4:
            gram_copy(k).wait_send()
    remote(rest, rest, send3.at[0], recv3, (i, s)).wait_send()
    few = region.at[:, :, pl.ds(0, OWN)]
    pl.when(jnp.logical_not(here))(
        lambda: remote(few, few, send3.at[1], recv3, (i, s)).wait_send()
    )
    remote(out, out, send3.at[0], recv3, (i, s)).wait_recv()


def on_device(fields, counts, cells, values, errors, radius):
    vmem = pl.BlockSpec(memory_space=pltpu.VMEM)
    smem = pl.BlockSpec(memory_space=pltpu.SMEM)
    hbm = pl.BlockSpec(memory_space=pl.ANY)
    dma = pltpu.SemaphoreType.DMA
    return pl.pallas_call(
        kernel,
        out_shape=jax.ShapeDtypeStruct(fields.shape, F32),
        in_specs=[hbm, vmem, vmem, vmem, smem, smem],
        out_specs=hbm,
        scratch_shapes=[
            pltpu.VMEM((OWN, 3, STRIPS * ROWS, BLOCK), F32),
            pltpu.VMEM((2, 2, 3, SPAN, COLS), F32),
            pltpu.VMEM((OWN, 2, 3, EDGE, COLS), F32),
            pltpu.VMEM((OWN, 2, 3, EDGE, COLS), F32),
            pltpu.VMEM((OWN, 3, STRIPS * ROWS, BLOCK), F32),
            pltpu.VMEM((3, ROWS, MEMBERS, COLS), F32),
            pltpu.VMEM((3, ROWS, MEMBERS, COLS), F32),
            pltpu.VMEM((8, OBS), F32),
            pltpu.VMEM((8, OBS), F32),
            pltpu.VMEM((8, COLS), F32),
            pltpu.VMEM((9, 8, COLS), F32),
            pltpu.VMEM((ROWS * COLS, OBS), BF16),
            pltpu.VMEM((OBS, COLS), BF16),
            pltpu.VMEM((OBS, COLS), BF16),
            pltpu.VMEM((2, MEMBERS, MEMBERS), F32),
            pltpu.VMEM((MEMBERS, COLS), BF16),
            pltpu.VMEM((MEMBERS, COLS), BF16),
            pltpu.VMEM((9, MEMBERS, COLS), F32),
            pltpu.VMEM((9, MEMBERS, COLS), F32),
            dma((OWN,)), dma((OWN,)), dma((OWN, 2)), dma((OWN, 2)), dma, dma, dma((10,)), dma, dma,
            dma((9,)), dma((9,)), dma((2,)), dma,
        ],
        compiler_params=pltpu.CompilerParams(
            has_side_effects=True, vmem_limit_bytes=40 * 1024 * 1024
        ),
        name="forecast_and_analysis",
    )(
        fields, cells.reshape(1, OBS), values.reshape(1, OBS), errors.reshape(1, OBS),
        counts, radius,
    )


def solution(mesh):
    in_specs = (
        P("member", None, "strip", None),
        P("strip", "member"),
        P("strip", "member", None),
        P("strip", "member", None),
        P("strip", "member", None),
        P("strip", "member"),
    )
    return jax.shard_map(
        on_device, mesh=mesh, in_specs=in_specs, out_specs=P("member", None, "strip", None),
        check_vma=False,
    )
```

time: 249 us -> 125 us (0.50)
  Pallas kernels: 0 us -> 119 us
  waiting for transfers between devices: 90.2 us -> 0 us
  other arithmetic: 47.4 us -> 0 us
  starting transfers between devices: 32.9 us -> 0 us
  blocking collectives: 29 us -> 0 us
  local copies, waits for them, and re-layouts: 31.8 us -> 4.58 us
  matrix products: 13.3 us -> 0 us
    pallas_call x0 -> x1, Pallas kernels: none -> 119 us  [on_device(): pl.pallas_call(kernel, out_shape=jax.ShapeDtypeStruct(fields.shape, F32),...]
    ppermute x12 -> x0, waiting for transfers between devices: 70.2 us -> none  [the longest x6 38.3 us: with_halo(): lax.ppermute(lax.slice_in_dim(block, block.shape[dim] - width, None, axis...]
    mul x22 -> x0, other arithmetic: 35 us -> none  [the longest x12 21.9 us: advance_once(): flux_x = column_depth * flow_x]
    all_to_all x1 -> x0, blocking collectives: 29 us -> none  [on_device(): lax.all_to_all(outgoing, 'member', split_axis=0, concat_axis=3, tiled=True)]
    ppermute x12 -> x0, starting transfers between devices: 23.4 us -> none  [the longest x6 19.1 us: with_halo(): lax.ppermute(lax.slice_in_dim(block, 0, width, axis=dim), axis, backward)]
    all_to_all x1 -> x0, waiting for transfers between devices: 19.9 us -> none  [on_device(): lax.all_to_all(by_block, 'member', split_axis=3, concat_axis=0, tiled=True)]
    dot_general x64 -> x0, matrix products: 13.3 us -> none  [the longest x20 3.26 us: analyse(): jnp.dot(inverse_root, iterate, precision=HIGHEST_PRECISION)]
    concatenate x5 -> x0, local copies, waits for them, and re-layouts: 12.9 us -> none  [the longest x4 12.9 us: strip_block(): jnp.concatenate([padded[..., -halo_depth:], padded, padded[..., :halo_dep...]
  transfers between devices with their start and end apart: 13 -> 0, of which waited for: 13 -> 0; matrix products, arithmetic and copies ran while one was open for 0% -> 0% of each run, Pallas kernels for 0% -> 0%
where the time goes in v1:
time: 125 us
  Pallas kernels  119 us (95%)
  local copies, waits for them, and re-layouts  4.58 us (4%)
  between operations  1.32 us (1%)
    pallas_call x1, Pallas kernels, on_device(): pl.pallas_call(kernel, out_shape=jax.ShapeDtypeStruct(fields.shape, F32),...  119 us
    unnamed x9, local copies, waits for them, and re-layouts  4.58 us

profile of v1, /device:TPU:1, one launch (start us, length us, event | category | flops | bytes accessed | tf_op | source)
XLA Modules:
  0.0 125.3 jit_solution(3008495371414236324)
XLA Ops:
  1.3 0.0 copy-start
  1.3 1.4 %copy-done = f32[4,3,16,2048]{3,2,1,0:T(8,128)S(1)} copy-done((f32[4,3,16,2048]{3,2,1,0:T(8,128)S(1)}, f32[4,3,16,2048]{3,2,1,0:T(8,128)}, u32[]{:S(2)}) %copy-start) | copy-done | bytes 1572888
  2.7 0.0 copy-start.1
  2.7 0.7 copy-done.1
  3.4 0.0 copy-start.2
  3.4 0.7 copy-done.2
  4.1 0.0 copy-start.3
  4.1 0.7 copy-done.3
  4.7 119.4 %forecast_and_analysis.1 = f32[4,3,16,2048]{3,2,1,0:T(8,128)S(1)} custom-call(f32[4,3,16,2048]{3,2,1,0:T(8,128)S(1)} %copy-done, s32[1,256]{1,0:T(1,128)S(1)} %bitcast.3, f32[1,256]{1,0:T(1,128)S(1)} %bitcast.4, f32[1,256]{1,0:T(1,128)S(1)} %bitcast.5, s32[1,1]{1,0:T(1,128)S(6)} %copy.8.count, s32[1,1]{1,0:T(1,128)S(6)} %copy.9.radius), custom_call_target="tpu_custom_call" | custom-call | tf_op jit(solution)/shard_map/forecast_and_analysis/pallas_call | solution.py:402
  124.1 1.1 copy.10
Async XLA Ops:
  1.3 1.4 %copy-start = (f32[4,3,16,2048]{3,2,1,0:T(8,128)S(1)}, f32[4,3,16,2048]{3,2,1,0:T(8,128)}, u32[]{:S(2)}) copy-start(f32[4,3,16,2048]{3,2,1,0:T(8,128)} %x.1) | copy-start | bytes 4718596
  2.7 0.7 copy-start.1
  3.4 0.7 copy-start.2
  4.1 0.7 copy-start.3

commit v2 on v1

--- a/solution.py
+++ b/solution.py
@@ -19,7 +19,6 @@
 GUARD = 8
 FIRST = GUARD + EDGE
 SPAN = BLOCK + 2 * EDGE + 2 * GUARD
-UNROLL = 6
 MESH = pl.DeviceIdType.MESH
 F32 = jnp.float32
 BF16 = jnp.bfloat16
@@ -93,7 +92,7 @@
     hn, hs = turn_north(h), turn_south(h)
     flow = (pe - pw) + (qn - qs)
     dst[0, rows] = (
-        (he * (0.25 - pe) + hw * (0.25 + pw)) + (turn_north(h * b) + turn_south(h * b2))
+        (he * (0.25 - pe) + hw * (0.25 + pw)) + (hn * (0.25 - qn) + hs * (0.25 + qs))
     ) - (1.0 / 64.0) * flow
     dst[1, rows] = ((a * pe + a2 * pw) + (b * pn + b2 * ps)) + (0.05 * q - (he - hw))
     dst[2, rows] = ((a * qe + a2 * qw) + (b * qn + b2 * qs)) - (0.05 * p + (hn - hs))
@@ -101,9 +100,9 @@
 
 def kernel(
     x, cells, values, errors, count, radius, out,
-    landed, work, edge, halo, staged, region, mixed, packed, own, reach, near, onehot, tall_h, tall_l, roots, mix_h, mix_l, gram,
+    raw_cells, raw, raw_scalars, raw_radius, landed, work, edge, halo, staged, region, mixed, packed, own, reach, near, onehot, tall_h, tall_l, roots, mix_h, mix_l, gram,
     grams,
-    send1, recv1, send_edge, recv_edge, send2, recv2, send_obs, recv_obs, recv_reach,
+    load_sem, send1, recv1, send_edge, recv_edge, send2, recv2, send_obs, recv_obs, recv_reach,
     send_gram, recv_gram, send3, recv3,
 ):
     i = lax.axis_index("member")
@@ -111,6 +110,44 @@
     t = block_of(s)
     a, b0 = region_of(i, s)
     b = 2 * t + b0
+
+    def neighbour(k):
+        return owner_of((a + 7 + k // 3) % 8, (b + 15 + k % 3) % 16)
+
+    to_i, to_s = owner_of(s, i)
+    mine = (to_i == i) & (to_s == s)
+    here = a == s
+    loads = [
+        pltpu.make_async_copy(cells, raw_cells, load_sem.at[0]),
+        pltpu.make_async_copy(values, raw.at[0:1], load_sem.at[1]),
+        pltpu.make_async_copy(errors, raw.at[1:2], load_sem.at[2]),
+        pltpu.make_async_copy(count, raw_scalars, load_sem.at[3]),
+        pltpu.make_async_copy(radius, raw_radius, load_sem.at[4]),
+    ]
+    for copy in loads:
+        copy.start()
+
+    barrier = pltpu.get_barrier_semaphore()
+
+    def greet(where):
+        pl.semaphore_signal(barrier, inc=1, device_id=where, device_id_type=MESH)
+
+    for k in range(9):
+        if k != 4:
+            greet(neighbour(k))
+    for n in range(OWNERS):
+        sender = owner_of(s, n)
+        pl.when((sender[0] != i) | (sender[1] != s))(lambda sender=sender: greet(sender))
+    pl.when((b != i) | (a != s))(lambda: greet((b, a)))
+    for d in range(1, OWNERS):
+        greet((lax.rem(i + d, OWNERS), s))
+    for d in range(1, STRIPS):
+        greet((i, lax.rem(s + d, STRIPS)))
+    pl.semaphore_wait(
+        barrier,
+        8 + OWNERS + 1 + (OWNERS - 1) + (STRIPS - 1)
+        - mine.astype(jnp.int32) - here.astype(jnp.int32),
+    )
 
     for j in range(OWN):
         for d in range(1, STRIPS):
@@ -126,13 +163,13 @@
             recv1.at[j],
         ).start()
 
+    for copy in loads:
+        copy.wait()
     slots = lax.broadcasted_iota(jnp.int32, (1, OBS), 1)
-    packed[0:1] = cells[...].astype(F32)
-    packed[1:2] = values[...]
-    packed[2:3] = jnp.where(slots < count[0, 0], 1.0 / errors[...], 0.0)
-    reach[...] = jnp.full((8, COLS), radius[0, 0], jnp.int32).astype(F32)
-    to_i, to_s = owner_of(s, i)
-    mine = (to_i == i) & (to_s == s)
+    packed[0:1] = raw_cells[...].astype(F32)
+    packed[1:2] = raw[0:1]
+    packed[2:3] = jnp.where(slots < raw_scalars[0:1, 0:1], 1.0 / raw[1:2], 0.0)
+    packed[3:4] = jnp.broadcast_to(raw_radius[0:1, 0:1].astype(F32), (1, OBS))
 
     @pl.when(mine)
     def _():
@@ -141,21 +178,6 @@
     @pl.when(jnp.logical_not(mine))
     def _():
         remote(packed, own, send_obs.at[9], recv_obs, (to_i, to_s)).start()
-
-    def each_near(act_local, act_remote):
-        for k in range(9):
-            n_i, n_s = owner_of((s + k // 3 + 7) % 8, (i + k % 3 + 15) % 16)
-            self = (n_i == i) & (n_s == s)
-            if act_local is not None:
-                pl.when(self)(lambda k=k: act_local(k))
-            pl.when(jnp.logical_not(self))(lambda k=k, n_i=n_i, n_s=n_s: act_remote(k, n_i, n_s))
-
-    each_near(
-        lambda k: pltpu.make_async_copy(reach, near.at[k], recv_reach).start(),
-        lambda k, n_i, n_s: remote(
-            reach, near.at[k], send_obs.at[k], recv_reach, (n_i, n_s)
-        ).start(),
-    )
 
     left = (i, strip_of((t + 7) % 8))
     right = (i, strip_of((t + 1) % 8))
@@ -199,13 +221,8 @@
             ping[f, FIRST + BLOCK : FIRST + BLOCK + EDGE] = halo[j, 1, f]
 
         def sweep(src, dst):
-            def chunk(n, _):
-                at = pl.multiple_of(n * (8 * UNROLL), 8) + GUARD
-                for u in range(UNROLL):
-                    step_rows(src, dst, at + 8 * u)
-                return 0
-
-            lax.fori_loop(0, (SPAN - 2 * GUARD) // (8 * UNROLL), chunk, 0)
+            for n in range((SPAN - 2 * GUARD) // 8):
+                step_rows(src, dst, GUARD + 8 * n)
 
         def two_steps(n, _):
             sweep(ping, pong)
@@ -231,9 +248,18 @@
             else:
                 remote(src, dst, send2, recv2, (to, s)).start()
 
+    def reach_copy(k):
+        return remote(
+            reach, near.at[k], send_obs.at[k], recv_reach.at[k], neighbour(k)
+        )
+
     arrive(0)
     arrive(1)
     pltpu.make_async_copy(own, own, recv_obs).wait()
+    reach[...] = jnp.broadcast_to(own[3:4, :COLS], (8, COLS))
+    for k in range(9):
+        if k != 4:
+            reach_copy(k).start()
     place = own[0:1]
 
     def mark(n, _):
@@ -272,7 +298,10 @@
     tall = jnp.concatenate([wide[:, :COLS].T, wide[:, COLS:].T], axis=0)
     columns_h, columns_l = halves(tall)
     tall_h[...], tall_l[...] = columns_h, columns_l
-    pltpu.make_async_copy(near, near, recv_reach).wait()
+    for k in range(9):
+        if k != 4:
+            reach_copy(k).wait_recv()
+    near[4] = reach[...]
 
     def product(k, _):
         r = row_pos + (k // 3 - 1).astype(F32)
@@ -286,8 +315,9 @@
     lax.fori_loop(0, 9, product, 0)
 
     def gram_copy(k):
-        to = owner_of((a + 9 - k // 3) % 8, (b + 17 - k % 3) % 16)
-        return remote(gram.at[k], grams.at[k], send_gram.at[k], recv_gram.at[k], to)
+        return remote(
+            gram.at[k], grams.at[k], send_gram.at[k], recv_gram.at[k], neighbour(8 - k)
+        )
 
     for k in range(9):
         if k != 4:
@@ -331,7 +361,6 @@
     weights_h, weights_l = halves(padded.T[:MEMBERS])
     mix_h[...], mix_l[...] = weights_h, weights_l
 
-    here = a == s
     columns = pl.ds(pl.multiple_of(b * COLS, COLS), COLS)
     for f in range(3):
 
@@ -375,12 +404,9 @@
     pl.when(jnp.logical_not(mine))(
         lambda: remote(packed, own, send_obs.at[9], recv_obs, (i, s)).wait_send()
     )
-    each_near(
-        None,
-        lambda k, n_i, n_s: remote(
-            reach, near.at[k], send_obs.at[k], recv_reach, (n_i, n_s)
-        ).wait_send(),
-    )
+    for k in range(9):
+        if k != 4:
+            reach_copy(k).wait_send()
     rest = region.at[:, :, pl.ds(0, OWN * (OWNERS - 1))]
     remote(rest, rest, send2, recv2, (i, s)).wait_send()
     for k in range(9):
@@ -395,16 +421,18 @@
 
 
 def on_device(fields, counts, cells, values, errors, radius):
-    vmem = pl.BlockSpec(memory_space=pltpu.VMEM)
-    smem = pl.BlockSpec(memory_space=pltpu.SMEM)
-    hbm = pl.BlockSpec(memory_space=pl.ANY)
+    hbm = pl.BlockSpec(memory_space=pltpu.HBM)
     dma = pltpu.SemaphoreType.DMA
     return pl.pallas_call(
         kernel,
         out_shape=jax.ShapeDtypeStruct(fields.shape, F32),
-        in_specs=[hbm, vmem, vmem, vmem, smem, smem],
-        out_specs=hbm,
+        in_specs=[hbm] * 6,
+        out_specs=pl.BlockSpec(memory_space=pl.ANY),
         scratch_shapes=[
+            pltpu.VMEM((1, OBS), jnp.int32),
+            pltpu.VMEM((2, OBS), F32),
+            pltpu.VMEM((1, 1), jnp.int32),
+            pltpu.VMEM((1, 1), jnp.int32),
             pltpu.VMEM((OWN, 3, STRIPS * ROWS, BLOCK), F32),
             pltpu.VMEM((2, 2, 3, SPAN, COLS), F32),
             pltpu.VMEM((OWN, 2, 3, EDGE, COLS), F32),
@@ -424,11 +452,12 @@
             pltpu.VMEM((MEMBERS, COLS), BF16),
             pltpu.VMEM((9, MEMBERS, COLS), F32),
             pltpu.VMEM((9, MEMBERS, COLS), F32),
-            dma((OWN,)), dma((OWN,)), dma((OWN, 2)), dma((OWN, 2)), dma, dma, dma((10,)), dma, dma,
+            dma((5,)), dma((OWN,)), dma((OWN,)), dma((OWN, 2)), dma((OWN, 2)), dma, dma,
+            dma((10,)), dma, dma((9,)),
             dma((9,)), dma((9,)), dma((2,)), dma,
         ],
         compiler_params=pltpu.CompilerParams(
-            has_side_effects=True, vmem_limit_bytes=40 * 1024 * 1024
+            collective_id=0, has_side_effects=True, vmem_limit_bytes=40 * 1024 * 1024
         ),
         name="forecast_and_analysis",
     )(

time: 125 us -> 102 us (0.82)
  Pallas kernels: 119 us -> 95.5 us
    pallas_call x1, Pallas kernels: 119 us -> 95.5 us  [on_device(): pl.pallas_call(kernel, out_shape=jax.ShapeDtypeStruct(fields.shape, F32),...]
where the time goes in v2:
time: 102 us; the launch traced here: 101 us
  Pallas kernels  95.5 us (94%)
  local copies, waits for them, and re-layouts  4.58 us (4%)
  between operations  1.32 us (1%)
    pallas_call x1, Pallas kernels, on_device(): pl.pallas_call(kernel, out_shape=jax.ShapeDtypeStruct(fields.shape, F32),...  95.5 us
    unnamed x9, local copies, waits for them, and re-layouts  4.58 us

profile of v2, /device:TPU:1, one launch (start us, length us, event | category | flops | bytes accessed | tf_op | source)
XLA Modules:
  0.0 101.4 jit_solution(13949877362664665465)
XLA Ops:
  1.3 0.0 copy-start
  1.3 1.4 %copy-done = f32[4,3,16,2048]{3,2,1,0:T(8,128)S(1)} copy-done((f32[4,3,16,2048]{3,2,1,0:T(8,128)S(1)}, f32[4,3,16,2048]{3,2,1,0:T(8,128)}, u32[]{:S(2)}) %copy-start) | copy-done | bytes 1572888
  2.7 0.0 copy-start.1
  2.7 0.7 copy-done.1
  3.4 0.0 copy-start.2
  3.4 0.7 copy-done.2
  4.1 0.0 copy-start.3
  4.1 0.7 copy-done.3
  4.7 95.5 %forecast_and_analysis.1 = f32[4,3,16,2048]{3,2,1,0:T(8,128)S(1)} custom-call(f32[4,3,16,2048]{3,2,1,0:T(8,128)S(1)} %copy-done, s32[1,256]{1,0:T(1,128)S(1)} %bitcast.3, f32[1,256]{1,0:T(1,128)S(1)} %bitcast.4, f32[1,256]{1,0:T(1,128)S(1)} %bitcast.5, s32[1,1]{1,0:T(1,128)S(6)} %copy.8.count, s32[1,1]{1,0:T(1,128)S(6)} %copy.9.radius), custom_call_target="tpu_custom_call" | custom-call | tf_op jit(solution)/shard_map/forecast_and_analysis/pallas_call | solution.py:426
  100.2 1.1 %copy.10 = f32[4,3,16,2048]{3,2,1,0:T(8,128)} copy(f32[4,3,16,2048]{3,2,1,0:T(8,128)S(1)} %forecast_and_analysis.1) | data formatting | bytes 3145728
Async XLA Ops:
  1.3 1.4 %copy-start = (f32[4,3,16,2048]{3,2,1,0:T(8,128)S(1)}, f32[4,3,16,2048]{3,2,1,0:T(8,128)}, u32[]{:S(2)}) copy-start(f32[4,3,16,2048]{3,2,1,0:T(8,128)} %x.1) | copy-start | bytes 4718596
  2.7 0.7 copy-start.1
  3.4 0.7 copy-start.2
  4.1 0.7 copy-start.3

commit v3 on v2

--- a/solution.py
+++ b/solution.py
@@ -24,24 +24,16 @@
 BF16 = jnp.bfloat16
 
 
-def block_of(strip):
-    z, xh = strip // 2, strip % 2
-    return z + xh * (7 - 2 * z)
-
-
-def strip_of(block):
-    return 2 * block + (block // 4) * (15 - 4 * block)
-
-
 def region_of(i, strip):
     y, c, z = (i // 2) % 4, i % 2, strip // 2
-    return 2 * ((y + z) % 4) + (c + y) % 2, i // 8
+    a = 2 * ((y + z) % 4) + (c + y) % 2
+    return a, (2 * strip + i // 8 + a % 2) % OWNERS
 
 
 def owner_of(a, b):
-    strip = strip_of(b // 2)
-    y = (a // 2 + 4 - strip // 2) % 4
-    return (b % 2) * 8 + y * 2 + (a + y) % 2, strip
+    first = (b + OWNERS - a % 2) % OWNERS
+    y = (a // 2 + 4 - first // 4) % 4
+    return (first % 2) * 8 + y * 2 + (a + y) % 2, first // 2
 
 
 def remote(src, dst, send, recv, where):
@@ -100,16 +92,15 @@
 
 def kernel(
     x, cells, values, errors, count, radius, out,
-    raw_cells, raw, raw_scalars, raw_radius, landed, work, edge, halo, staged, region, mixed, packed, own, reach, near, onehot, tall_h, tall_l, roots, mix_h, mix_l, gram,
+    raw_cells, raw, raw_scalars, raw_radius, held, landed, work, edge, edges, halo, staged, region, mixed, packed, own, reach, near, onehot, roots, mix_h, mix_l, gram,
     grams,
     load_sem, send1, recv1, send_edge, recv_edge, send2, recv2, send_obs, recv_obs, recv_reach,
     send_gram, recv_gram, send3, recv3,
 ):
     i = lax.axis_index("member")
     s = lax.axis_index("strip")
-    t = block_of(s)
-    a, b0 = region_of(i, s)
-    b = 2 * t + b0
+    a, b = region_of(i, s)
+    shift = i // 8
 
     def neighbour(k):
         return owner_of((a + 7 + k // 3) % 8, (b + 15 + k % 3) % 16)
@@ -126,6 +117,8 @@
     ]
     for copy in loads:
         copy.start()
+    own_input = pltpu.make_async_copy(x, held, load_sem.at[5])
+    own_input.start()
 
     barrier = pltpu.get_barrier_semaphore()
 
@@ -140,7 +133,8 @@
         pl.when((sender[0] != i) | (sender[1] != s))(lambda sender=sender: greet(sender))
     pl.when((b != i) | (a != s))(lambda: greet((b, a)))
     for d in range(1, OWNERS):
-        greet((lax.rem(i + d, OWNERS), s))
+        n = lax.rem(i + d, OWNERS)
+        greet((n, ((b + OWNERS - n // 8) % OWNERS) // 2))
     for d in range(1, STRIPS):
         greet((i, lax.rem(s + d, STRIPS)))
     pl.semaphore_wait(
@@ -148,20 +142,6 @@
         8 + OWNERS + 1 + (OWNERS - 1) + (STRIPS - 1)
         - mine.astype(jnp.int32) - here.astype(jnp.int32),
     )
-
-    for j in range(OWN):
-        for d in range(1, STRIPS):
-            to = lax.rem(s + d, STRIPS)
-            remote(
-                x.at[j, :, :, pl.ds(pl.multiple_of(block_of(to) * BLOCK, BLOCK), BLOCK)],
-                landed.at[j, :, pl.ds(pl.multiple_of(s * ROWS, ROWS), ROWS)],
-                send1.at[j], recv1.at[j], (i, to),
-            ).start()
-        pltpu.make_async_copy(
-            x.at[j, :, :, pl.ds(pl.multiple_of(t * BLOCK, BLOCK), BLOCK)],
-            landed.at[j, :, pl.ds(pl.multiple_of(s * ROWS, ROWS), ROWS)],
-            recv1.at[j],
-        ).start()
 
     for copy in loads:
         copy.wait()
@@ -179,46 +159,75 @@
     def _():
         remote(packed, own, send_obs.at[9], recv_obs, (to_i, to_s)).start()
 
-    left = (i, strip_of((t + 7) % 8))
-    right = (i, strip_of((t + 1) % 8))
-    for c in range(2):
-        for g in range(2):
-            for f in range(3):
-                work[c, g, f, 0:GUARD] = jnp.zeros((GUARD, COLS), F32)
-                work[c, g, f, SPAN - GUARD : SPAN] = jnp.zeros((GUARD, COLS), F32)
-
-    def edge_copies(j):
-        return (
-            remote(
-                edge.at[j, 0], halo.at[j, 1], send_edge.at[j, 0], recv_edge.at[j, 1], left
-            ),
-            remote(
-                edge.at[j, 1], halo.at[j, 0], send_edge.at[j, 1], recv_edge.at[j, 0], right
-            ),
-        )
+    def columns_of(strip, n):
+        return pl.ds(pl.multiple_of(((2 * strip + shift + n) % OWNERS) * COLS, COLS), COLS)
+
+    strip_rows = pl.ds(pl.multiple_of(s * ROWS, ROWS), ROWS)
+
+    def send_member(j):
+        for d in range(1, STRIPS):
+            to = lax.rem(s + d, STRIPS)
+            for h in range(2):
+                remote(
+                    held.at[j, :, :, columns_of(to, h)],
+                    landed.at[j, :, strip_rows, pl.ds(h * COLS, COLS)],
+                    send1.at[j], recv1.at[j], (i, to),
+                ).start()
+
+    own_input.wait()
+    send_member(0)
+    for j in range(OWN):
+        for h in range(2):
+            pltpu.make_async_copy(
+                x.at[j, :, :, columns_of(s, h)],
+                landed.at[j, :, strip_rows, pl.ds(h * COLS, COLS)],
+                recv1.at[j],
+            ).start()
+    lanes = lax.broadcasted_iota(jnp.int32, (ROWS, COLS), 1)
+
+    def pack_edges(to, _):
+        for f in range(3):
+            joined = jnp.zeros((ROWS, COLS), F32)
+            for j in range(OWN):
+                both = jnp.where(
+                    lanes < COLS // 2,
+                    held[j, f, :, columns_of(to, 2)],
+                    held[j, f, :, columns_of(to, OWNERS - 1)],
+                )
+                turned = pltpu.roll(both, j * 2 * EDGE + EDGE, 1)
+                joined = jnp.where(lanes // (2 * EDGE) == j, turned, joined)
+            edge[to, f] = joined
+        return 0
+
+    lax.fori_loop(0, STRIPS, pack_edges, 0)
+    for d in range(1, STRIPS):
+        to = lax.rem(s + d, STRIPS)
+        remote(
+            edge.at[to], edges.at[:, strip_rows], send_edge, recv_edge, (i, to)
+        ).start()
+    for j in range(1, OWN):
+        send_member(j)
+    edges[:, strip_rows] = edge[s]
+
+    for g in range(2):
+        for f in range(3):
+            work[g, f, 0:GUARD] = jnp.zeros((GUARD, COLS), F32)
+            work[g, f, SPAN - GUARD : SPAN] = jnp.zeros((GUARD, COLS), F32)
+    ping, pong = work.at[0], work.at[1]
 
     def arrive(j):
         pltpu.make_async_copy(landed.at[j], landed.at[j], recv1.at[j]).wait()
-        buf = work.at[j % 2, 0]
         for f in range(3):
             scale = 1.0 / 64.0 if f == 0 else 0.125
             for c in range(2):
                 turned = landed[j, f, :, c * COLS : (c + 1) * COLS].T * scale
-                buf[f, FIRST + c * COLS : FIRST + (c + 1) * COLS] = turned
-                if c == 0:
-                    edge[j, 0, f] = turned[:EDGE]
-                else:
-                    edge[j, 1, f] = turned[COLS - EDGE :]
-        for copy in edge_copies(j):
-            copy.start()
+                ping[f, FIRST + c * COLS : FIRST + (c + 1) * COLS] = turned
 
     def forecast(j):
-        for copy in edge_copies(j):
-            copy.wait_recv()
-        ping, pong = work.at[j % 2, 0], work.at[j % 2, 1]
         for f in range(3):
-            ping[f, GUARD:FIRST] = halo[j, 0, f]
-            ping[f, FIRST + BLOCK : FIRST + BLOCK + EDGE] = halo[j, 1, f]
+            low, mid, high = (2 * j) * EDGE, (2 * j + 1) * EDGE, (2 * j + 2) * EDGE
+            ping[f, GUARD:FIRST] = halo[f, low:mid]
+            ping[f, FIRST + BLOCK : FIRST + BLOCK + EDGE] = halo[f, mid:high]
 
         def sweep(src, dst):
             for n in range((SPAN - 2 * GUARD) // 8):
@@ -235,26 +244,26 @@
             for c in range(2):
                 block = ping[f, FIRST + c * COLS : FIRST + (c + 1) * COLS]
                 staged[j, f, :, c * COLS : (c + 1) * COLS] = block.T * scale
-        for d in range(OWNERS):
-            to = lax.rem(i + d, OWNERS)
-            to_a, to_b0 = region_of(to, s)
-            src = staged.at[
-                j, :, pl.ds(pl.multiple_of(to_a * ROWS, ROWS), ROWS),
-                pl.ds(pl.multiple_of(to_b0 * COLS, COLS), COLS),
-            ]
-            dst = region.at[:, :, OWN * i + j]
-            if d == 0:
-                pltpu.make_async_copy(src, dst, recv2).start()
-            else:
-                remote(src, dst, send2, recv2, (to, s)).start()
+        for d in range(STRIPS):
+            to_a = lax.rem(a + d, STRIPS)
+            for e in range(2):
+                n = (to_a + d + e) % 2
+                src = staged.at[
+                    j, :, pl.ds(pl.multiple_of(to_a * ROWS, ROWS), ROWS),
+                    pl.ds(pl.multiple_of(n * COLS, COLS), COLS),
+                ]
+                dst = region.at[:, :, OWN * i + j]
+                if d == 0 and e == 0:
+                    pltpu.make_async_copy(src, dst, recv2).start()
+                else:
+                    to = owner_of(to_a, (2 * s + shift + n) % OWNERS)
+                    remote(src, dst, send2, recv2, to).start()
 
     def reach_copy(k):
         return remote(
             reach, near.at[k], send_obs.at[k], recv_reach.at[k], neighbour(k)
         )
 
-    arrive(0)
-    arrive(1)
     pltpu.make_async_copy(own, own, recv_obs).wait()
     reach[...] = jnp.broadcast_to(own[3:4, :COLS], (8, COLS))
     for k in range(9):
@@ -269,12 +278,15 @@
         return 0
 
     lax.fori_loop(0, ROWS, mark, 0)
+    arrive(0)
+    rest = edges.at[:, pl.ds(0, ROWS * (STRIPS - 1))]
+    remote(rest, rest, send_edge, recv_edge, (i, s)).wait_recv()
+    for f in range(3):
+        halo[f] = edges[f].T * (1.0 / 64.0 if f == 0 else 0.125)
     forecast(0)
-    arrive(2)
-    forecast(1)
-    arrive(3)
-    forecast(2)
-    forecast(3)
+    for j in range(1, OWN):
+        arrive(j)
+        forecast(j)
 
     pltpu.make_async_copy(region, region, recv2).wait()
 
@@ -297,29 +309,22 @@
     )
     tall = jnp.concatenate([wide[:, :COLS].T, wide[:, COLS:].T], axis=0)
     columns_h, columns_l = halves(tall)
-    tall_h[...], tall_l[...] = columns_h, columns_l
     for k in range(9):
         if k != 4:
             reach_copy(k).wait_recv()
     near[4] = reach[...]
-
-    def product(k, _):
-        r = row_pos + (k // 3 - 1).astype(F32)
-        c = col_pos + (k % 3 - 1).astype(F32)
-        radius_k = near[k, 0:1, 0:1]
-        taper = jnp.exp(-0.5 * (r * r + c * c) / (radius_k * radius_k))
-        wh, wl = halves(spread * (taper * precision))
-        gram[k] = dot(wh, tall_h[...]) + (dot(wh, tall_l[...]) + dot(wl, tall_h[...]))
-        return 0
-
-    lax.fori_loop(0, 9, product, 0)
 
     def gram_copy(k):
         return remote(
             gram.at[k], grams.at[k], send_gram.at[k], recv_gram.at[k], neighbour(8 - k)
         )
 
-    for k in range(9):
+    for k in (0, 1, 2, 3, 5, 6, 7, 8, 4):
+        r, c = row_pos + (k // 3 - 1.0), col_pos + (k % 3 - 1.0)
+        radius_k = near[k, 0:1, 0:1]
+        taper = jnp.exp(-0.5 * (r * r + c * c) / (radius_k * radius_k))
+        wh, wl = halves(spread * (taper * precision))
+        gram[k] = dot(wh, columns_h) + (dot(wh, columns_l) + dot(wl, columns_h))
         if k != 4:
             gram_copy(k).start()
     total = gram[4]
@@ -399,8 +404,8 @@
     for j in range(OWN):
         rest = landed.at[j, :, pl.ds(0, ROWS * (STRIPS - 1))]
         remote(rest, rest, send1.at[j], recv1.at[j], (i, s)).wait_send()
-        for copy in edge_copies(j):
-            copy.wait_send()
+    rest = edges.at[:, pl.ds(0, ROWS * (STRIPS - 1))]
+    remote(rest, rest, send_edge, recv_edge, (i, s)).wait_send()
     pl.when(jnp.logical_not(mine))(
         lambda: remote(packed, own, send_obs.at[9], recv_obs, (i, s)).wait_send()
     )
@@ -433,10 +438,12 @@
             pltpu.VMEM((2, OBS), F32),
             pltpu.VMEM((1, 1), jnp.int32),
             pltpu.VMEM((1, 1), jnp.int32),
+            pltpu.VMEM((OWN, 3, ROWS, 2048), F32),
             pltpu.VMEM((OWN, 3, STRIPS * ROWS, BLOCK), F32),
-            pltpu.VMEM((2, 2, 3, SPAN, COLS), F32),
-            pltpu.VMEM((OWN, 2, 3, EDGE, COLS), F32),
-            pltpu.VMEM((OWN, 2, 3, EDGE, COLS), F32),
+            pltpu.VMEM((2, 3, SPAN, COLS), F32),
+            pltpu.VMEM((STRIPS, 3, ROWS, COLS), F32),
+            pltpu.VMEM((3, STRIPS * ROWS, COLS), F32),
+            pltpu.VMEM((3, STRIPS * ROWS, COLS), F32),
             pltpu.VMEM((OWN, 3, STRIPS * ROWS, BLOCK), F32),
             pltpu.VMEM((3, ROWS, MEMBERS, COLS), F32),
             pltpu.VMEM((3, ROWS, MEMBERS, COLS), F32),
@@ -445,19 +452,17 @@
             pltpu.VMEM((8, COLS), F32),
             pltpu.VMEM((9, 8, COLS), F32),
             pltpu.VMEM((ROWS * COLS, OBS), BF16),
-            pltpu.VMEM((OBS, COLS), BF16),
-            pltpu.VMEM((OBS, COLS), BF16),
             pltpu.VMEM((2, MEMBERS, MEMBERS), F32),
             pltpu.VMEM((MEMBERS, COLS), BF16),
             pltpu.VMEM((MEMBERS, COLS), BF16),
             pltpu.VMEM((9, MEMBERS, COLS), F32),
             pltpu.VMEM((9, MEMBERS, COLS), F32),
-            dma((5,)), dma((OWN,)), dma((OWN,)), dma((OWN, 2)), dma((OWN, 2)), dma, dma,
+            dma((6,)), dma((OWN,)), dma((OWN,)), dma, dma, dma, dma,
             dma((10,)), dma, dma((9,)),
             dma((9,)), dma((9,)), dma((2,)), dma,
         ],
         compiler_params=pltpu.CompilerParams(
-            collective_id=0, has_side_effects=True, vmem_limit_bytes=40 * 1024 * 1024
+            collective_id=0, has_side_effects=True, vmem_limit_bytes=67043328
         ),
         name="forecast_and_analysis",
     )(

time: 102 us -> 89.4 us (0.88)
  Pallas kernels: 95.5 us -> 85.3 us
  local copies, waits for them, and re-layouts: 4.58 us -> 2.7 us
    pallas_call x1, Pallas kernels: 95.5 us -> 85.3 us  [on_device(): pl.pallas_call(kernel, out_shape=jax.ShapeDtypeStruct(fields.shape, F32),...]
    unnamed x9 -> x1, local copies, waits for them, and re-layouts: 4.58 us -> 2.7 us
where the time goes in v3:
time: 89.4 us; the launch traced here: 89.3 us
  Pallas kernels  85.3 us (95%)
  local copies, waits for them, and re-layouts  2.7 us (3%)
  between operations  1.3 us (1%)
    pallas_call x1, Pallas kernels, on_device(): pl.pallas_call(kernel, out_shape=jax.ShapeDtypeStruct(fields.shape, F32),...  85.3 us
    unnamed x1, local copies, waits for them, and re-layouts  2.7 us

profile of v3, /device:TPU:1, one launch (start us, length us, event | category | flops | bytes accessed | tf_op | source)
XLA Modules:
  0.0 89.3 jit_solution(14880434793721527353)
XLA Ops:
  1.3 85.3 %forecast_and_analysis.1 = f32[4,3,16,2048]{3,2,1,0:T(8,128)} custom-call(f32[4,3,16,2048]{3,2,1,0:T(8,128)} %x.1, s32[1,256]{1,0:T(1,128)} %bitcast.3, f32[1,256]{1,0:T(1,128)} %bitcast.4, f32[1,256]{1,0:T(1,128)} %bitcast.5, s32[1,1]{1,0:T(1,128)S(6)} %copy.8.count, s32[1,1]{1,0:T(1,128)S(6)} %copy.9.radius), custom_call_target="tpu_custom_call" | custom-call | tf_op jit(solution)/shard_map/forecast_and_analysis/pallas_call | solution.py:431
  86.6 2.7 %copy.10 = f32[4,3,16,2048]{3,2,1,0:T(8,128)} copy(f32[4,3,16,2048]{3,2,1,0:T(8,128)} %forecast_and_analysis.1) | data formatting | bytes 3145728

commit v4 on v3

--- a/solution.py
+++ b/solution.py
@@ -92,7 +92,7 @@
 
 def kernel(
     x, cells, values, errors, count, radius, out,
-    raw_cells, raw, raw_scalars, raw_radius, held, landed, work, edge, edges, halo, staged, region, mixed, packed, own, reach, near, onehot, roots, mix_h, mix_l, gram,
+    raw_cells, raw, raw_scalars, raw_radius, held, landed, work, edge, edges, halo, staged, region, mixed, packed, own, reach, near, onehot, observed, roots, mix_h, mix_l, gram,
     grams,
     load_sem, send1, recv1, send_edge, recv_edge, send2, recv2, send_obs, recv_obs, recv_reach,
     send_gram, recv_gram, send3, recv3,
@@ -244,20 +244,23 @@
             for c in range(2):
                 block = ping[f, FIRST + c * COLS : FIRST + (c + 1) * COLS]
                 staged[j, f, :, c * COLS : (c + 1) * COLS] = block.T * scale
+
+    def send_fields(j, low, high):
         for d in range(STRIPS):
             to_a = lax.rem(a + d, STRIPS)
             for e in range(2):
                 n = (to_a + d + e) % 2
                 src = staged.at[
-                    j, :, pl.ds(pl.multiple_of(to_a * ROWS, ROWS), ROWS),
+                    j, low:high, pl.ds(pl.multiple_of(to_a * ROWS, ROWS), ROWS),
                     pl.ds(pl.multiple_of(n * COLS, COLS), COLS),
                 ]
-                dst = region.at[:, :, OWN * i + j]
+                dst = region.at[low:high, :, OWNERS * j + i]
+                done = recv2.at[j if low == 0 else OWN]
                 if d == 0 and e == 0:
-                    pltpu.make_async_copy(src, dst, recv2).start()
+                    pltpu.make_async_copy(src, dst, done).start()
                 else:
                     to = owner_of(to_a, (2 * s + shift + n) % OWNERS)
-                    remote(src, dst, send2, recv2, to).start()
+                    remote(src, dst, send2, done, to).start()
 
     def reach_copy(k):
         return remote(
@@ -284,19 +287,35 @@
     for f in range(3):
         halo[f] = edges[f].T * (1.0 / 64.0 if f == 0 else 0.125)
     forecast(0)
-    for j in range(1, OWN):
-        arrive(j)
-        forecast(j)
-
-    pltpu.make_async_copy(region, region, recv2).wait()
-
-    def look(n, height):
-        pair = jnp.concatenate([region[0, 2 * n], region[0, 2 * n + 1]], axis=1)
-        marks = onehot[pl.ds(pl.multiple_of(n * OBS, OBS), OBS)]
-        high, mid, low = thirds(pair)
-        return height + (dot(high, marks) + (dot(mid, marks) + dot(low, marks)))
-
-    height = lax.fori_loop(0, ROWS // 2, look, jnp.zeros((MEMBERS, OBS), F32))
+    send_fields(0, 0, 1)
+    send_fields(0, 1, 3)
+    arrive(1)
+    forecast(1)
+    send_fields(1, 0, 1)
+    send_fields(1, 1, 3)
+    arrive(2)
+    forecast(2)
+    send_fields(2, 0, 1)
+    arrive(3)
+    forecast(3)
+    send_fields(3, 0, 1)
+
+    for j in range(OWN):
+        group = slice(OWNERS * j, OWNERS * (j + 1))
+        some = region.at[0, :, group]
+        pltpu.make_async_copy(some, some, recv2.at[j]).wait()
+        found = jnp.zeros((OWNERS, OBS), F32)
+        for n in range(8):
+            pair = jnp.concatenate(
+                [region[0, 2 * n, group], region[0, 2 * n + 1, group]], axis=1
+            )
+            marks = onehot[n * OBS : (n + 1) * OBS]
+            part = dot(jnp.concatenate(thirds(pair), axis=0), marks)
+            found = found + (
+                part[:OWNERS] + (part[OWNERS : 2 * OWNERS] + part[2 * OWNERS :])
+            )
+        observed[group] = found
+    height = observed[...]
     mean = jnp.mean(height, axis=0, keepdims=True)
     spread = height - mean
     innovation = own[1:2] - mean
@@ -319,14 +338,26 @@
             gram.at[k], grams.at[k], send_gram.at[k], recv_gram.at[k], neighbour(8 - k)
         )
 
-    for k in (0, 1, 2, 3, 5, 6, 7, 8, 4):
+    weighted_h, weighted_l = [], []
+    for k in range(9):
         r, c = row_pos + (k // 3 - 1.0), col_pos + (k % 3 - 1.0)
         radius_k = near[k, 0:1, 0:1]
         taper = jnp.exp(-0.5 * (r * r + c * c) / (radius_k * radius_k))
         wh, wl = halves(spread * (taper * precision))
-        gram[k] = dot(wh, columns_h) + (dot(wh, columns_l) + dot(wl, columns_h))
+        weighted_h.append(wh)
+        weighted_l.append(wl)
+    weighted_h = jnp.concatenate(weighted_h, axis=0)
+    weighted_l = jnp.concatenate(weighted_l, axis=0)
+    products = dot(weighted_h, columns_h) + (
+        dot(weighted_h, columns_l) + dot(weighted_l, columns_h)
+    )
+    for k in range(9):
+        gram[k] = products[k * MEMBERS : (k + 1) * MEMBERS]
+    for k in range(9):
         if k != 4:
             gram_copy(k).start()
+    send_fields(2, 1, 3)
+    send_fields(3, 1, 3)
     total = gram[4]
     for k in range(9):
         if k != 4:
@@ -367,7 +398,10 @@
     mix_h[...], mix_l[...] = weights_h, weights_l
 
     columns = pl.ds(pl.multiple_of(b * COLS, COLS), COLS)
+    flows = region.at[1:3]
     for f in range(3):
+        if f == 1:
+            pltpu.make_async_copy(flows, flows, recv2.at[OWN]).wait()
 
         def rows_of(n, _):
             pair = jnp.concatenate([region[f, 2 * n], region[f, 2 * n + 1]], axis=1)
@@ -385,7 +419,7 @@
         for d in range(OWNERS):
             to = lax.rem(i + d, OWNERS)
             for j in range(OWN):
-                src = mixed.at[f, :, OWN * to + j]
+                src = mixed.at[f, :, OWNERS * j + to]
                 dst = out.at[j, f, :, columns]
                 if d == 0:
                     pl.when(here)(
@@ -413,7 +447,7 @@
         if k != 4:
             reach_copy(k).wait_send()
     rest = region.at[:, :, pl.ds(0, OWN * (OWNERS - 1))]
-    remote(rest, rest, send2, recv2, (i, s)).wait_send()
+    remote(rest, rest, send2, recv2.at[0], (i, s)).wait_send()
     for k in range(9):
         if k != 4:
             gram_copy(k).wait_send()
@@ -452,21 +486,27 @@
             pltpu.VMEM((8, COLS), F32),
             pltpu.VMEM((9, 8, COLS), F32),
             pltpu.VMEM((ROWS * COLS, OBS), BF16),
+            pltpu.VMEM((MEMBERS, OBS), F32),
             pltpu.VMEM((2, MEMBERS, MEMBERS), F32),
             pltpu.VMEM((MEMBERS, COLS), BF16),
             pltpu.VMEM((MEMBERS, COLS), BF16),
             pltpu.VMEM((9, MEMBERS, COLS), F32),
             pltpu.VMEM((9, MEMBERS, COLS), F32),
-            dma((6,)), dma((OWN,)), dma((OWN,)), dma, dma, dma, dma,
+            dma((6,)), dma((OWN,)), dma((OWN,)), dma, dma, dma, dma((OWN + 1,)),
             dma((10,)), dma, dma((9,)),
             dma((9,)), dma((9,)), dma((2,)), dma,
         ],
         compiler_params=pltpu.CompilerParams(
-            collective_id=0, has_side_effects=True, vmem_limit_bytes=67043328
+            collective_id=0, has_side_effects=True, vmem_limit_bytes=40 * 1024 * 1024
         ),
         name="forecast_and_analysis",
     )(
-        fields, cells.reshape(1, OBS), values.reshape(1, OBS), errors.reshape(1, OBS),
+        *(
+            pltpu.with_memory_space_constraint(operand, pltpu.HBM)
+            for operand in (
+                fields, cells.reshape(1, OBS), values.reshape(1, OBS), errors.reshape(1, OBS),
+            )
+        ),
         counts, radius,
     )
 

time: 89.4 us -> 83.5 us (0.934)
  Pallas kernels: 85.3 us -> 81 us
  local copies, waits for them, and re-layouts: 2.7 us -> 1.15 us
    pallas_call x1, Pallas kernels: 85.3 us -> 81 us  [on_device(): pl.pallas_call(kernel, out_shape=jax.ShapeDtypeStruct(fields.shape, F32),...]
    unnamed x1, local copies, waits for them, and re-layouts: 2.7 us -> 1.15 us
where the time goes in v4:
time: 83.5 us; the launch traced here: 83.4 us
  Pallas kernels  81 us (97%)
  between operations  1.3 us (2%)
  local copies, waits for them, and re-layouts  1.15 us (1%)
    pallas_call x1, Pallas kernels, on_device(): pl.pallas_call(kernel, out_shape=jax.ShapeDtypeStruct(fields.shape, F32),...  81 us

profile of v4, /device:TPU:1, one launch (start us, length us, event | category | flops | bytes accessed | tf_op | source)
XLA Modules:
  0.0 83.4 jit_solution(5699196879340505071)
XLA Ops:
  1.3 81.0 %forecast_and_analysis.1 = f32[4,3,16,2048]{3,2,1,0:T(8,128)S(1)} custom-call(f32[4,3,16,2048]{3,2,1,0:T(8,128)} %x.1, s32[1,256]{1,0:T(1,128)} %bitcast.3, f32[1,256]{1,0:T(1,128)} %bitcast.4, f32[1,256]{1,0:T(1,128)} %bitcast.5, s32[1,1]{1,0:T(1,128)S(6)} %copy.8.count, s32[1,1]{1,0:T(1,128)S(6)} %copy.9.radius), custom_call_target="tpu_custom_call" | custom-call | tf_op jit(solution)/shard_map/forecast_and_analysis/pallas_call | solution.py:465
  82.3 1.1 %copy.10 = f32[4,3,16,2048]{3,2,1,0:T(8,128)} copy(f32[4,3,16,2048]{3,2,1,0:T(8,128)S(1)} %forecast_and_analysis.1) | data formatting | bytes 3145728

commit v5 on v4

--- a/solution.py
+++ b/solution.py
@@ -8,6 +8,7 @@
 STEPS = 12
 TURNS = 20
 MEMBERS = 64
+HALF = MEMBERS // 2
 OWN = 4
 STRIPS = 8
 OWNERS = 16
@@ -223,28 +224,6 @@
                 turned = landed[j, f, :, c * COLS : (c + 1) * COLS].T * scale
                 ping[f, FIRST + c * COLS : FIRST + (c + 1) * COLS] = turned
 
-    def forecast(j):
-        for f in range(3):
-            low, mid, high = (2 * j) * EDGE, (2 * j + 1) * EDGE, (2 * j + 2) * EDGE
-            ping[f, GUARD:FIRST] = halo[f, low:mid]
-            ping[f, FIRST + BLOCK : FIRST + BLOCK + EDGE] = halo[f, mid:high]
-
-        def sweep(src, dst):
-            for n in range((SPAN - 2 * GUARD) // 8):
-                step_rows(src, dst, GUARD + 8 * n)
-
-        def two_steps(n, _):
-            sweep(ping, pong)
-            sweep(pong, ping)
-            return 0
-
-        lax.fori_loop(0, STEPS // 2, two_steps, 0)
-        for f in range(3):
-            scale = 64.0 if f == 0 else 8.0
-            for c in range(2):
-                block = ping[f, FIRST + c * COLS : FIRST + (c + 1) * COLS]
-                staged[j, f, :, c * COLS : (c + 1) * COLS] = block.T * scale
-
     def send_fields(j, low, high):
         for d in range(STRIPS):
             to_a = lax.rem(a + d, STRIPS)
@@ -262,6 +241,30 @@
                     to = owner_of(to_a, (2 * s + shift + n) % OWNERS)
                     remote(src, dst, send2, done, to).start()
 
+    def forecast(j):
+        for f in range(3):
+            low, mid, high = (2 * j) * EDGE, (2 * j + 1) * EDGE, (2 * j + 2) * EDGE
+            ping[f, GUARD:FIRST] = halo[f, low:mid]
+            ping[f, FIRST + BLOCK : FIRST + BLOCK + EDGE] = halo[f, mid:high]
+
+        def sweep(src, dst):
+            for n in range((SPAN - 2 * GUARD) // 8):
+                step_rows(src, dst, GUARD + 8 * n)
+
+        def two_steps(n, _):
+            sweep(ping, pong)
+            sweep(pong, ping)
+            return 0
+
+        lax.fori_loop(0, STEPS // 2, two_steps, 0)
+        for f in range(3):
+            scale = 64.0 if f == 0 else 8.0
+            for c in range(2):
+                block = ping[f, FIRST + c * COLS : FIRST + (c + 1) * COLS]
+                staged[j, f, :, c * COLS : (c + 1) * COLS] = block.T * scale
+            if f == 0:
+                send_fields(j, 0, 1)
+
     def reach_copy(k):
         return remote(
             reach, near.at[k], send_obs.at[k], recv_reach.at[k], neighbour(k)
@@ -287,18 +290,14 @@
     for f in range(3):
         halo[f] = edges[f].T * (1.0 / 64.0 if f == 0 else 0.125)
     forecast(0)
-    send_fields(0, 0, 1)
     send_fields(0, 1, 3)
     arrive(1)
     forecast(1)
-    send_fields(1, 0, 1)
     send_fields(1, 1, 3)
     arrive(2)
     forecast(2)
-    send_fields(2, 0, 1)
     arrive(3)
     forecast(3)
-    send_fields(3, 0, 1)
 
     for j in range(OWN):
         group = slice(OWNERS * j, OWNERS * (j + 1))
@@ -323,9 +322,7 @@
     line = jnp.floor(place * (1.0 / COLS))
     row_pos = (line + 0.5) * (1.0 / ROWS) - 0.5
     col_pos = (place - line * COLS + 0.5) * (1.0 / COLS) - 0.5
-    wide = jnp.concatenate(
-        [spread, innovation, jnp.zeros((COLS - MEMBERS - 1, OBS), F32)], axis=0
-    )
+    wide = jnp.concatenate([spread, jnp.zeros((COLS - MEMBERS, OBS), F32)], axis=0)
     tall = jnp.concatenate([wide[:, :COLS].T, wide[:, COLS:].T], axis=0)
     columns_h, columns_l = halves(tall)
     for k in range(9):
@@ -338,21 +335,32 @@
             gram.at[k], grams.at[k], send_gram.at[k], recv_gram.at[k], neighbour(8 - k)
         )
 
-    weighted_h, weighted_l = [], []
+    weighted_h, weighted_l, pulls = [], [], []
     for k in range(9):
         r, c = row_pos + (k // 3 - 1.0), col_pos + (k % 3 - 1.0)
         radius_k = near[k, 0:1, 0:1]
         taper = jnp.exp(-0.5 * (r * r + c * c) / (radius_k * radius_k))
-        wh, wl = halves(spread * (taper * precision))
+        weight = taper * precision
+        wh, wl = halves(spread * weight)
         weighted_h.append(wh)
         weighted_l.append(wl)
+        pulls.append(innovation * weight)
+    wh, wl = halves(jnp.concatenate(pulls + [jnp.zeros((7, OBS), F32)], axis=0))
+    weighted_h.append(wh)
+    weighted_l.append(wl)
     weighted_h = jnp.concatenate(weighted_h, axis=0)
     weighted_l = jnp.concatenate(weighted_l, axis=0)
     products = dot(weighted_h, columns_h) + (
         dot(weighted_h, columns_l) + dot(weighted_l, columns_h)
     )
     for k in range(9):
-        gram[k] = products[k * MEMBERS : (k + 1) * MEMBERS]
+        at = k * MEMBERS
+        gram[k, :HALF] = products[at : at + HALF] + pltpu.roll(
+            products[at + HALF : at + MEMBERS], MEMBERS, 1
+        )
+        gram[k, HALF:] = jnp.broadcast_to(
+            products[9 * MEMBERS + k : 9 * MEMBERS + k + 1], (8, COLS)
+        )
     for k in range(9):
         if k != 4:
             gram_copy(k).start()
@@ -369,7 +377,9 @@
         lax.broadcasted_iota(jnp.int32, (MEMBERS, MEMBERS), 0)
         == lax.broadcasted_iota(jnp.int32, (MEMBERS, MEMBERS), 1)
     ).astype(F32)
-    normal = eye + total[:, :MEMBERS] * scale
+    upper = total[:HALF]
+    lower = pltpu.roll(upper, MEMBERS, 1)
+    normal = eye + jnp.concatenate([upper[:, :MEMBERS], lower[:, :MEMBERS]], axis=0) * scale
     frob2 = jnp.sum(jnp.sum(normal * normal, axis=1, keepdims=True), axis=0, keepdims=True)
     frob = jnp.sqrt(frob2)
 
@@ -383,18 +393,16 @@
 
     lax.fori_loop(0, TURNS, turn, 0)
     inverse = roots[1]
-    pull = matmul(inverse, matmul(inverse, total)) / frob
-    lane = lax.broadcasted_iota(jnp.int32, (MEMBERS, COLS), 1)
-    mean_weights = jnp.sum(jnp.where(lane == MEMBERS, pull, 0.0), axis=1, keepdims=True) * scale
-    transform = inverse / jnp.sqrt(frob) + mean_weights
     padded = jnp.concatenate(
         [
-            jnp.concatenate([transform, jnp.zeros((MEMBERS, MEMBERS), F32)], axis=1),
+            jnp.concatenate([inverse, jnp.zeros((MEMBERS, MEMBERS), F32)], axis=1),
             jnp.zeros((MEMBERS, COLS), F32),
         ],
         axis=0,
     )
-    weights_h, weights_l = halves(padded.T[:MEMBERS])
+    turned = padded.T[:MEMBERS, :MEMBERS]
+    pull = matmul(matmul(total[HALF:, :MEMBERS], turned), turned) / frob
+    weights_h, weights_l = halves(turned / jnp.sqrt(frob) + pull[0:1] * scale)
     mix_h[...], mix_l[...] = weights_h, weights_l
 
     columns = pl.ds(pl.multiple_of(b * COLS, COLS), COLS)
@@ -408,19 +416,22 @@
             centre = jnp.mean(pair, axis=0, keepdims=True)
             dev_h, dev_l = halves(pair - centre)
             result = centre + (
-                dot(mix_h[:, :MEMBERS], dev_h)
-                + (dot(mix_h[:, :MEMBERS], dev_l) + dot(mix_l[:, :MEMBERS], dev_h))
+                dot(mix_h[...], dev_h)
+                + (dot(mix_h[...], dev_l) + dot(mix_l[...], dev_h))
             )
             mixed[f, 2 * n] = result[:, :COLS]
             mixed[f, 2 * n + 1] = result[:, COLS:]
             return 0
 
         lax.fori_loop(0, ROWS // 2, rows_of, 0)
+        if f == 1:
+            continue
+        low, high = (0, 1) if f == 0 else (1, 3)
         for d in range(OWNERS):
             to = lax.rem(i + d, OWNERS)
             for j in range(OWN):
-                src = mixed.at[f, :, OWNERS * j + to]
-                dst = out.at[j, f, :, columns]
+                src = mixed.at[low:high, :, OWNERS * j + to]
+                dst = out.at[j, low:high, :, columns]
                 if d == 0:
                     pl.when(here)(
                         lambda src=src, dst=dst: pltpu.make_async_copy(
@@ -488,10 +499,10 @@
             pltpu.VMEM((ROWS * COLS, OBS), BF16),
             pltpu.VMEM((MEMBERS, OBS), F32),
             pltpu.VMEM((2, MEMBERS, MEMBERS), F32),
-            pltpu.VMEM((MEMBERS, COLS), BF16),
-            pltpu.VMEM((MEMBERS, COLS), BF16),
-            pltpu.VMEM((9, MEMBERS, COLS), F32),
-            pltpu.VMEM((9, MEMBERS, COLS), F32),
+            pltpu.VMEM((MEMBERS, MEMBERS), BF16),
+            pltpu.VMEM((MEMBERS, MEMBERS), BF16),
+            pltpu.VMEM((9, HALF + 8, COLS), F32),
+            pltpu.VMEM((9, HALF + 8, COLS), F32),
             dma((6,)), dma((OWN,)), dma((OWN,)), dma, dma, dma, dma((OWN + 1,)),
             dma((10,)), dma, dma((9,)),
             dma((9,)), dma((9,)), dma((2,)), dma,

time: 83.5 us -> 82.5 us (0.988)
  Pallas kernels: 81 us -> 79.9 us
    pallas_call x1, Pallas kernels: 81 us -> 79.9 us  [on_device(): pl.pallas_call(kernel, out_shape=jax.ShapeDtypeStruct(fields.shape, F32),...]
where the time goes in v5:
time: 82.5 us; the launch traced here: 82.4 us
  Pallas kernels  79.9 us (97%)
  between operations  1.3 us (2%)
  local copies, waits for them, and re-layouts  1.15 us (1%)
    pallas_call x1, Pallas kernels, on_device(): pl.pallas_call(kernel, out_shape=jax.ShapeDtypeStruct(fields.shape, F32),...  79.9 us

profile of v5, /device:TPU:1, one launch (start us, length us, event | category | flops | bytes accessed | tf_op | source)
XLA Modules:
  0.0 82.4 jit_solution(18246315447916472138)
XLA Ops:
  1.3 79.9 %forecast_and_analysis.1 = f32[4,3,16,2048]{3,2,1,0:T(8,128)S(1)} custom-call(f32[4,3,16,2048]{3,2,1,0:T(8,128)} %x.1, s32[1,256]{1,0:T(1,128)} %bitcast.3, f32[1,256]{1,0:T(1,128)} %bitcast.4, f32[1,256]{1,0:T(1,128)} %bitcast.5, s32[1,1]{1,0:T(1,128)S(6)} %copy.8.count, s32[1,1]{1,0:T(1,128)S(6)} %copy.9.radius), custom_call_target="tpu_custom_call" | custom-call | tf_op jit(solution)/shard_map/forecast_and_analysis/pallas_call | solution.py:476
  81.2 1.1 %copy.10 = f32[4,3,16,2048]{3,2,1,0:T(8,128)} copy(f32[4,3,16,2048]{3,2,1,0:T(8,128)S(1)} %forecast_and_analysis.1) | data formatting | bytes 3145728

commit v6 on v5

--- a/solution.py
+++ b/solution.py
@@ -387,11 +387,13 @@
 
     def turn(_, carry):
         u, z = roots[0], roots[1]
-        factor = 1.5 * eye - 0.5 * matmul(z, u)
-        roots[0], roots[1] = matmul(u, factor), matmul(factor, z)
+        for _ in range(2):
+            factor = 1.5 * eye - 0.5 * matmul(z, u)
+            u, z = matmul(u, factor), matmul(factor, z)
+        roots[0], roots[1] = u, z
         return carry
 
-    lax.fori_loop(0, TURNS, turn, 0)
+    lax.fori_loop(0, TURNS // 2, turn, 0)
     inverse = roots[1]
     padded = jnp.concatenate(
         [

time: 82.5 us -> 82.3 us (level)
  no operation moved by 1% of the time
where the time goes in v6:
time: 82.3 us; the launch traced here: 82.2 us
  Pallas kernels  79.7 us (97%)
  between operations  1.3 us (2%)
  local copies, waits for them, and re-layouts  1.15 us (1%)
    pallas_call x1, Pallas kernels, on_device(): pl.pallas_call(kernel, out_shape=jax.ShapeDtypeStruct(fields.shape, F32),...  79.7 us

profile of v6, /device:TPU:1, one launch (start us, length us, event | category | flops | bytes accessed | tf_op | source)
XLA Modules:
  0.0 82.2 jit_solution(5856774533105792676)
XLA Ops:
  1.3 79.7 %forecast_and_analysis.1 = f32[4,3,16,2048]{3,2,1,0:T(8,128)S(1)} custom-call(f32[4,3,16,2048]{3,2,1,0:T(8,128)} %x.1, s32[1,256]{1,0:T(1,128)} %bitcast.3, f32[1,256]{1,0:T(1,128)} %bitcast.4, f32[1,256]{1,0:T(1,128)} %bitcast.5, s32[1,1]{1,0:T(1,128)S(6)} %copy.8.count, s32[1,1]{1,0:T(1,128)S(6)} %copy.9.radius), custom_call_target="tpu_custom_call" | custom-call | tf_op jit(solution)/shard_map/forecast_and_analysis/pallas_call | solution.py:478
  81.0 1.1 %copy.10 = f32[4,3,16,2048]{3,2,1,0:T(8,128)} copy(f32[4,3,16,2048]{3,2,1,0:T(8,128)S(1)} %forecast_and_analysis.1) | data formatting | bytes 3145728
